TPU v7x, 32 devices: a whole 2x2x4 slice. The times are simulated.
32 devices in a mesh: dp: 8 (over z, x), tensor: 4 (over y, core).
Axes of the slice: x: 2, y: 2, z: 4, core: 2. Of those that a mesh axis runs over, the one named last changes fastest.
Arguments:
- tokens: bfloat16 [24576, 1024], P(('dp', 'tensor'))
- cotangent: bfloat16 [24576, 1024], P(('dp', 'tensor')), may hold values from -6 to 6
- image_ids: int32 [24576], P('dp'), may hold values from -1 to 15, as said below
- attn_master: float32 [4, 1024, 1024], P(None, 'dp', 'tensor')
- attn_first: float32 [4, 1024, 1024], P(None, 'dp', 'tensor'), may hold values from -256 to 256
- attn_second: float32 [4, 1024, 1024], P(None, 'dp', 'tensor'), may hold values from 245.76 to 7372.8
- mlp_master: float32 [2, 1024, 4096], P(None, 'dp', 'tensor'), may hold values from -0.1875 to 0.1875
- mlp_first: float32 [2, 1024, 4096], P(None, 'dp', 'tensor'), may hold values from -256 to 256
- mlp_second: float32 [2, 1024, 4096], P(None, 'dp', 'tensor'), may hold values from 245.76 to 7372.8
- vectors: float32 [14, 1024], replicated
- vector_first: float32 [14, 1024], replicated, may hold values from -256 to 256
- vector_second: float32 [14, 1024], replicated, may hold values from 245.76 to 7372.8
Outputs:
- block_out: bfloat16 [24576, 1024], P(('dp', 'tensor'))
- grad_tokens: float32 [24576, 1024], P(('dp', 'tensor'))
- attn_grad: float32 [4, 1024, 1024], P(None, 'dp', 'tensor')
- attn_new: float32 [4, 1024, 1024], P(None, 'dp', 'tensor')
- attn_first_new: float32 [4, 1024, 1024], P(None, 'dp', 'tensor')
- attn_second_new: float32 [3, 1024, 1024], P(None, 'dp', 'tensor')
- out_second_new: float32 [1024, 1024], P('dp', 'tensor')
- attn_copy: bfloat16 [4, 1024, 1024], P(None, 'dp', 'tensor')
- mlp_grad: float32 [2, 1024, 4096], P(None, 'dp', 'tensor')
- mlp_new: float32 [2, 1024, 4096], P(None, 'dp', 'tensor')
- mlp_first_new: float32 [2, 1024, 4096], P(None, 'dp', 'tensor')
- mlp_second_new: float32 [2, 1024, 4096], P(None, 'dp', 'tensor')
- mlp_copy: bfloat16 [2, 1024, 4096], P(None, 'dp', 'tensor')
- vector_grad: float32 [14, 1024], replicated
- vector_new: float32 [14, 1024], replicated
- vector_first_new: float32 [14, 1024], replicated
- vector_second_new: float32 [14, 1024], replicated
- vector_copy: bfloat16 [14, 1024], replicated
- matrix_norms: float32 [2, 6], replicated
- row_rms: float32 [4], replicated
Inputs may be any that keep to these rules, and one draw needn't show every extreme that they name: `image_ids`: every 3072 consecutive tokens hold, from their start, 1 to 2 whole images of 1370 tokens each, then padding; some group holds 2 images; every image has a number of its own.
All inputs are finite; a program needn't handle non-finite values.
Results may differ from a plain program's by a relative error of at most 0.008.
The roundings to bfloat16 on the way count: a program that leaves them out, or rounds other values in their place, can miss the bound.
Values may be sent and summed in bfloat16 or wider, within the bound.
A program may use at most 256 MiB of HBM per device.

v0:
```python
import jax
import jax.numpy as jnp
from jax import lax
from jax.sharding import PartitionSpec as P

HEAD_DIM = 64
QBLOCK = 512
STEP = 3


beta_rate = 0.5
adam_epsilon = 1e-06
norm_epsilon = 1e-06
learning_rate = 0.5
vector_rate = 0.05
weight_decay = 0.05
masked_score = -1e30


def layer_norm(values, gain, shift):
    average = jnp.mean(values, axis=-1, keepdims=True)
    centered = values - average
    variance = jnp.mean(centered * centered, axis=-1, keepdims=True)
    return centered * lax.rsqrt(variance + norm_epsilon) * gain + shift


def gelu_exact(values):
    return jax.nn.gelu(values, approximate=False)


def gather_rows(values):
    return lax.all_gather(values, "tensor", axis=0, tiled=True)


def sum_product(left_operand, right_operand):
    return lax.psum_scatter(
        jnp.einsum("sgk,sdk->gd", left_operand, right_operand, preferred_element_type=jnp.float32),
        "tensor",
        scatter_dimension=0,
        tiled=True,
    )


def split_heads(matrix):
    return matrix.reshape(matrix.shape[0], matrix.shape[1] // HEAD_DIM, HEAD_DIM)


def block_scores(query_heads, key_heads, group_ids, block_start):
    total_rows = group_ids.shape[0]
    block_query = lax.dynamic_slice_in_dim(query_heads, block_start, QBLOCK, 0)
    block_ids = lax.dynamic_slice_in_dim(group_ids, block_start, QBLOCK, 0)
    row_position = block_start + jnp.arange(QBLOCK)
    column_position = jnp.arange(total_rows)
    same_image = (block_ids[:, None] == group_ids[None, :]) & (block_ids[:, None] >= 0)
    allowed = same_image | (row_position[:, None] == column_position[None, :])
    scores = jnp.einsum(
        "bhd,khd->hbk", block_query, key_heads, preferred_element_type=jnp.float32
    ) * HEAD_DIM ** (-0.5)
    return (jnp.where(allowed[None], scores, masked_score), allowed, block_query)


def attend_forward(query_heads, key_heads, value_heads, group_ids):
    total_rows = query_heads.shape[0]
    block_total = total_rows // QBLOCK

    def one_block(block_index):
        scores, allowed, block_query = block_scores(
            query_heads, key_heads, group_ids, block_index * QBLOCK
        )
        largest = jnp.max(scores, axis=-1, keepdims=True)
        raised = jnp.exp(scores - largest)
        totals = jnp.sum(raised, axis=-1, keepdims=True)
        probs = (raised / totals).astype(jnp.bfloat16)
        output = jnp.einsum("hbk,khd->bhd", probs, value_heads, preferred_element_type=jnp.float32)
        return (output, (largest + jnp.log(totals))[..., 0])

    outputs, logsum = lax.map(one_block, jnp.arange(block_total))
    return (outputs.reshape(total_rows, -1), logsum)


def attend_backward(query_heads, key_heads, value_heads, group_ids, logsum, grad_heads):
    total_rows = query_heads.shape[0]
    block_total = total_rows // QBLOCK
    scale = HEAD_DIM ** (-0.5)

    def one_block(carried, block_index):
        grad_keys, grad_values = carried
        block_start = block_index * QBLOCK
        scores, allowed, block_query = block_scores(query_heads, key_heads, group_ids, block_start)
        block_grad = lax.dynamic_slice_in_dim(grad_heads, block_start, QBLOCK, 0)
        soft = jnp.where(allowed[None], jnp.exp(scores - logsum[block_index][..., None]), 0.0)
        grad_soft = jnp.einsum(
            "bhd,khd->hbk", block_grad, value_heads, preferred_element_type=jnp.float32
        )
        inner = jnp.sum(soft * grad_soft, axis=-1, keepdims=True)
        grad_scores = (soft * (grad_soft - inner)).astype(jnp.bfloat16)
        grad_query = (
            jnp.einsum("hbk,khd->bhd", grad_scores, key_heads, preferred_element_type=jnp.float32)
            * scale
        ).astype(jnp.bfloat16)
        grad_keys = (
            grad_keys
            + jnp.einsum(
                "hbk,bhd->khd", grad_scores, block_query, preferred_element_type=jnp.float32
            )
            * scale
        )
        grad_values = grad_values + jnp.einsum(
            "hbk,bhd->khd",
            soft.astype(jnp.bfloat16),
            block_grad,
            preferred_element_type=jnp.float32,
        )
        return ((grad_keys, grad_values), grad_query)

    zero_heads = jnp.zeros(query_heads.shape, jnp.float32)
    (grad_keys, grad_values), grad_query = lax.scan(
        one_block, (zero_heads, zero_heads), jnp.arange(block_total)
    )
    return jnp.stack(
        [
            grad_query.reshape(total_rows, -1),
            grad_keys.reshape(total_rows, -1).astype(jnp.bfloat16),
            grad_values.reshape(total_rows, -1).astype(jnp.bfloat16),
        ]
    )


def adapt_moments(gradient, first, second):
    new_first = beta_rate * first + (1.0 - beta_rate) * gradient
    new_second = beta_rate * second + (1.0 - beta_rate) * gradient * gradient
    first_hat = new_first / (1.0 - beta_rate**STEP)
    second_hat = new_second / (1.0 - beta_rate**STEP)
    return (new_first, new_second, first_hat / (jnp.sqrt(second_hat) + adam_epsilon))


def per_device(
    tokens,
    cotangent,
    image_ids,
    attn_master,
    attn_first,
    attn_second,
    mlp_master,
    mlp_first,
    mlp_second,
    vectors,
    vector_first,
    vector_second,
):
    local_rows = tokens.shape[0]
    model_width = tokens.shape[1]
    tensor_rank = lax.axis_index("tensor")
    attn_full, mlp_full = (
        lax.all_gather(attn_master.astype(jnp.bfloat16), "dp", axis=1, tiled=True),
        lax.all_gather(mlp_master.astype(jnp.bfloat16), "dp", axis=1, tiled=True),
    )
    head_width = attn_full.shape[2]
    hidden_width = mlp_full.shape[2]
    head_start = tensor_rank * head_width
    hidden_start = tensor_rank * hidden_width
    local_ids = lax.dynamic_slice_in_dim(image_ids, tensor_rank * local_rows, local_rows, 0)
    valid = (local_ids >= 0).astype(jnp.float32)[:, None]
    up_bias = vectors[10:].reshape(-1)
    bias_slices = lax.dynamic_slice_in_dim(vectors[2:4], head_start, head_width, 1)
    up_slice = lax.dynamic_slice_in_dim(up_bias, hidden_start, hidden_width, 0)
    inputs = tokens.astype(jnp.float32)
    normed_one = gather_rows(layer_norm(inputs, vectors[0], vectors[1]).astype(jnp.bfloat16))
    projected = jnp.einsum(
        "gd,sdk->sgk", normed_one, attn_full[:3], preferred_element_type=jnp.float32
    )
    projected = (
        projected
        + jnp.stack([bias_slices[0], jnp.zeros_like(bias_slices[0]), bias_slices[1]])[:, None, :]
    )
    qkv_low = projected.astype(jnp.bfloat16)
    query_heads = split_heads(qkv_low[0])
    key_heads = split_heads(qkv_low[1])
    value_heads = split_heads(qkv_low[2])
    attended, logsum = attend_forward(query_heads, key_heads, value_heads, image_ids)
    mixed = attended.astype(jnp.bfloat16)
    attn_out = sum_product(mixed[None], attn_full[3:4])
    branch_one = (attn_out + vectors[4]) * vectors[5]
    middle = inputs + branch_one
    normed_two = gather_rows(layer_norm(middle, vectors[6], vectors[7]).astype(jnp.bfloat16))
    upper_input = jnp.dot(normed_two, mlp_full[0], preferred_element_type=jnp.float32) + up_slice
    hidden = gelu_exact(upper_input).astype(jnp.bfloat16)
    down_output = sum_product(hidden[None], mlp_full[1:2])
    branch_two = (down_output + vectors[8]) * vectors[9]
    result = middle + branch_two
    stat_terms = jnp.stack(
        [
            jnp.sum(valid),
            jnp.sum(valid * middle * middle),
            jnp.sum(valid * branch_one * branch_one),
            jnp.sum(valid * result * result),
            jnp.sum(valid * branch_two * branch_two),
        ]
    )
    weight_local_sq = jnp.concatenate(
        [
            jnp.sum(attn_master * attn_master, axis=(1, 2)),
            jnp.sum(mlp_master * mlp_master, axis=(1, 2)),
        ]
    )
    row_totals = lax.psum(stat_terms, ("dp", "tensor"))
    seed_grad = cotangent.astype(jnp.float32) * valid
    grad_scale_two = jnp.sum(seed_grad * (down_output + vectors[8]), axis=0)
    grad_bias_down = jnp.sum(seed_grad * vectors[9], axis=0)
    grad_down = gather_rows((seed_grad * vectors[9]).astype(jnp.bfloat16))
    grad_down_weight = jnp.einsum(
        "gd,gf->df", grad_down, hidden, preferred_element_type=jnp.float32
    )
    grad_hidden = jnp.dot(grad_down, mlp_full[1], preferred_element_type=jnp.float32)
    gelu_value, gelu_back = jax.vjp(gelu_exact, upper_input)
    grad_upper = gelu_back(grad_hidden)[0].astype(jnp.bfloat16)
    grad_up_bias = jnp.sum(grad_upper.astype(jnp.float32), axis=0)
    grad_up_weight = jnp.einsum(
        "gd,gf->df", normed_two, grad_upper, preferred_element_type=jnp.float32
    )
    mlp_grad_full = jnp.stack([grad_up_weight, grad_down_weight])
    grad_normed_two = sum_product(grad_upper[None], mlp_full[0:1])
    norm_value_two, norm_back_two = jax.vjp(layer_norm, middle, vectors[6], vectors[7])
    grad_middle_part, grad_gain_two, grad_shift_two = norm_back_two(grad_normed_two)
    grad_middle = seed_grad + grad_middle_part
    grad_scale_one = jnp.sum(grad_middle * (attn_out + vectors[4]), axis=0)
    grad_bias_out = jnp.sum(grad_middle * vectors[5], axis=0)
    grad_attn_out = gather_rows((grad_middle * vectors[5]).astype(jnp.bfloat16))
    grad_out_weight = jnp.einsum(
        "gd,gk->dk", grad_attn_out, mixed, preferred_element_type=jnp.float32
    )
    grad_mixed = jnp.dot(grad_attn_out, attn_full[3], preferred_element_type=jnp.float32).astype(
        jnp.bfloat16
    )
    grad_heads = attend_backward(
        query_heads, key_heads, value_heads, image_ids, logsum, split_heads(grad_mixed)
    )
    grad_attn_full = jnp.concatenate(
        [
            jnp.einsum("gd,sgk->sdk", normed_one, grad_heads, preferred_element_type=jnp.float32),
            grad_out_weight[None],
        ],
        axis=0,
    )
    grad_bias_query = jnp.sum(grad_heads[0].astype(jnp.float32), axis=0)
    grad_bias_value = jnp.sum(grad_heads[2].astype(jnp.float32), axis=0)
    grad_normed_one = sum_product(grad_heads, attn_full[:3])
    norm_value_one, norm_back_one = jax.vjp(layer_norm, inputs, vectors[0], vectors[1])
    grad_input_part, grad_gain_one, grad_shift_one = norm_back_one(grad_normed_one)
    grad_tokens = grad_middle + grad_input_part
    zero_row = jnp.zeros((model_width,), jnp.float32)
    query_bias_row = lax.dynamic_update_slice_in_dim(zero_row, grad_bias_query, head_start, 0)
    value_bias_row = lax.dynamic_update_slice_in_dim(zero_row, grad_bias_value, head_start, 0)
    up_rows = lax.dynamic_update_slice_in_dim(
        jnp.zeros(up_bias.shape, jnp.float32), grad_up_bias, hidden_start, 0
    ).reshape(-1, model_width)
    vector_grad_local = jnp.concatenate(
        [
            jnp.stack(
                [
                    grad_gain_one,
                    grad_shift_one,
                    query_bias_row,
                    value_bias_row,
                    grad_bias_out,
                    grad_scale_one,
                    grad_gain_two,
                    grad_shift_two,
                    grad_bias_down,
                    grad_scale_two,
                ]
            ),
            up_rows,
        ],
        axis=0,
    )
    vector_total = lax.psum(vector_grad_local, ("dp", "tensor"))
    attn_shard, mlp_shard = (
        lax.psum_scatter(grad_attn_full, "dp", scatter_dimension=1, tiled=True),
        lax.psum_scatter(mlp_grad_full, "dp", scatter_dimension=1, tiled=True),
    )
    attn_first_new, attn_second_new, attn_adapted = adapt_moments(
        attn_shard, attn_first, attn_second
    )
    mlp_first_new, mlp_second_new, mlp_adapted = adapt_moments(mlp_shard, mlp_first, mlp_second)
    attn_update = attn_adapted + weight_decay * attn_master
    mlp_update = mlp_adapted + weight_decay * mlp_master
    update_local_sq = jnp.concatenate(
        [
            jnp.sum(attn_update * attn_update, axis=(1, 2)),
            jnp.sum(mlp_update * mlp_update, axis=(1, 2)),
        ]
    )
    weight_sq, update_sq = lax.psum((weight_local_sq, update_local_sq), ("dp", "tensor"))
    weight_norms = jnp.sqrt(weight_sq)
    update_norms = jnp.sqrt(update_sq)
    ratios = weight_norms / update_norms
    attn_new = attn_master - learning_rate * ratios[:4, None, None] * attn_update
    mlp_new = mlp_master - learning_rate * ratios[4:, None, None] * mlp_update
    vector_first_new, vector_second_new, vector_adapted = adapt_moments(
        vector_total, vector_first, vector_second
    )
    vector_new = vectors - vector_rate * vector_adapted
    matrix_norms = jnp.stack([weight_norms, update_norms])
    row_rms = jnp.sqrt(row_totals[1:] / (row_totals[0] * model_width))
    return (
        result.astype(jnp.bfloat16),
        grad_tokens,
        attn_shard,
        attn_new,
        attn_first_new,
        attn_second_new[:3],
        attn_second_new[3],
        attn_new.astype(jnp.bfloat16),
        mlp_shard,
        mlp_new,
        mlp_first_new,
        mlp_second_new,
        mlp_new.astype(jnp.bfloat16),
        vector_total,
        vector_new,
        vector_first_new,
        vector_second_new,
        vector_new.astype(jnp.bfloat16),
        matrix_norms,
        row_rms,
    )


def solution(mesh):
    in_specs = (
        P(("dp", "tensor"), None),
        P(("dp", "tensor"), None),
        P("dp"),
        P(None, "dp", "tensor"),
        P(None, "dp", "tensor"),
        P(None, "dp", "tensor"),
        P(None, "dp", "tensor"),
        P(None, "dp", "tensor"),
        P(None, "dp", "tensor"),
        P(),
        P(),
        P(),
    )
    out_specs = (
        P(("dp", "tensor"), None),
        P(("dp", "tensor"), None),
        P(None, "dp", "tensor"),
        P(None, "dp", "tensor"),
        P(None, "dp", "tensor"),
        P(None, "dp", "tensor"),
        P("dp", "tensor"),
        P(None, "dp", "tensor"),
        P(None, "dp", "tensor"),
        P(None, "dp", "tensor"),
        P(None, "dp", "tensor"),
        P(None, "dp", "tensor"),
        P(None, "dp", "tensor"),
        P(),
        P(),
        P(),
        P(),
        P(),
        P(),
        P(),
    )
    return jax.shard_map(
        per_device, mesh=mesh, in_specs=in_specs, out_specs=out_specs, check_vma=False
    )
```

profile of v0, /device:TPU:0, one launch (start us, length us, event | category | flops | bytes accessed | tf_op | source)
XLA Modules:
  0.0 1764.3 jit_solution(836512826943716215)
XLA Ops:
  14.3 49.4 %all-gather.9.cloned.1.call-done = bf16[4,1024,256]{1,2,0:T(8,128)(2,1)} async-done(((bf16[4,128,256]{1,2,0:T(8,128)(2,1)}), bf16[4,1024,256]{1,2,0:T(8,128)(2,1)}) %all-gather.9.cloned.1.call-update) | async-done | bytes 2097168 | tf_op jit(solution)/shard_map/all_gather | solution.py:155
  63.7 46.7 %all-gather.7.cloned.1.call-done = bf16[3072,1024]{1,0:T(8,128)(2,1)} async-done(((bf16[768,1024]{1,0:T(8,128)(2,1)}), bf16[3072,1024]{1,0:T(8,128)(2,1)}) %all-gather.7.cloned.1.call-update) | async-done | bytes 6291472 | tf_op jit(solution)/shard_map/all_gather | solution.py:32
  119.7 245.4 %while.27 = (s32[]{:T(128)}, bf16[6,512,4,64]{1,3,2,0:T(8,128)(2,1)}, f32[6,4,512]{2,1,0:T(4,128)}, s32[6]{0:T(128)S(1)}, s32[3072]{0:T(1024)S(1)}, /*index=5*/b...) while((s32[]{:T(128)}, ...), condition=%wide.region_5.6_spmd, body=%wide.region_2.5_spmd.sunk | while | flops 1692400640 | bytes 85810376 | solution.py:77
  123.5 12.3 fusion.143
  135.8 11.9 fusion.144
  147.7 12.3 fusion.145
  164.3 12.3 fusion.143
  176.7 11.9 fusion.144
  188.5 12.3 fusion.145
  205.2 12.3 fusion.143
  217.5 11.9 fusion.144
  229.4 12.3 fusion.145
  246.1 12.3 fusion.143
  258.4 11.9 fusion.144
  270.3 12.3 fusion.145
  287.0 12.3 fusion.143
  299.3 11.9 fusion.144
  311.2 12.3 fusion.145
  327.8 12.3 fusion.143
  340.1 11.9 fusion.144
  352.0 12.3 fusion.145
  380.1 97.6 %reduce-scatter.7.cloned.1.call-done = f32[768,1024]{1,0:T(8,128)} async-done(((f32[3072,1024]{1,0:T(8,128)}), f32[768,1024]{1,0:T(8,128)}) %reduce-scatter.7.cloned.1.call-update) | async-done | bytes 3145744 | tf_op jit(solution)/shard_map/reduce_scatter | solution.py:36
  486.7 66.3 %all-gather.13.cloned.1.call-done = bf16[2,1024,1024]{2,1,0:T(8,128)(2,1)} async-done(((bf16[2,128,1024]{2,1,0:T(8,128)(2,1)}), bf16[2,1024,1024]{2,1,0:T(8,128)(2,1)}) %all-gather.13.cloned.1.call-update) | async-done | bytes 4194320 | tf_op jit(solution)/shard_map/all_gather | solution.py:156
  553.1 46.9 %all-gather.11.cloned.1.call-done = bf16[3072,1024]{1,0:T(8,128)(2,1)} async-done(((bf16[768,1024]{1,0:T(8,128)(2,1)}), bf16[3072,1024]{1,0:T(8,128)(2,1)}) %all-gather.11.cloned.1.call-update) | async-done | bytes 6291472 | tf_op jit(solution)/shard_map/all_gather | solution.py:32
  600.0 37.2 %multiply_convert_fusion.1 = (bf16[3072,1024]{1,0:T(8,128)(2,1)S(1)}, f32[3072,1024]{1,0:T(8,128)}, f32[3072,1024]{1,0:T(8,128)}) fusion(f32[1024]{0:T(1024)S(1)} %dynamic_slice.35, bf16[3072,1024]{1,0:T(8,128)(2,1)} %all-gather.11.cloned.1.call-done, bf16[2,1024,1024]{2,1,0:T(8,128)(2,1)} %all-gather.13.cloned.1.call-done), kind=kOutput, calls=%fused_computation.50 | convolution fusion | flops 6650068992 | bytes 39849984 | tf_op jit(solution)/shard_map/dot_general | solution.py:186
  649.1 24.6 %convert_reduce_fusion = (f32[1024]{0:T(1024)}, bf16[3072,1024]{1,0:T(8,128)(2,1)}) fusion(f32[3072,1024]{1,0:T(8,128)} %get-tuple-element.288, bf16[3072,1024]{1,0:T(8,128)(2,1)} %all-gather.15.cloned.1.call-done, bf16[2,1024,1024]{2,1,0:T(8,128)(2,1)} %all-gather.13.cloned.1.call-done, f32[3072,1024]{1,0:T(8,128)} %get-tuple-element.313, ...), kind=kOutput, calls=%fused_computation.48 | convolution fusion | flops 6495927296 | bytes 39854080 | tf_op jit(solution)/shard_map/dot_general | solution.py:214
  673.7 12.5 fusion.70
  686.3 63.8 %reduce-scatter.9.cloned.1.call-done = f32[768,1024]{1,0:T(8,128)} async-done(((f32[3072,1024]{1,0:T(8,128)}), f32[768,1024]{1,0:T(8,128)}) %reduce-scatter.9.cloned.1.call-update) | async-done | bytes 3145744 | tf_op jit(solution)/shard_map/reduce_scatter | solution.py:36
  750.0 102.2 %reduce-scatter.11.cloned.1.call-done = f32[768,1024]{1,0:T(8,128)} async-done(((f32[3072,1024]{1,0:T(8,128)}), f32[768,1024]{1,0:T(8,128)}) %reduce-scatter.11.cloned.1.call-update) | async-done | bytes 3145744 | tf_op jit(solution)/shard_map/reduce_scatter | solution.py:36
  867.9 10.7 convolution_bitcast_fusion.1
  878.6 10.8 convolution_bitcast_fusion.2
  893.6 20.8 %all-gather.17.cloned.1.call-done = bf16[3072,1024]{1,0:T(8,128)(2,1)} async-done(((bf16[768,1024]{1,0:T(8,128)(2,1)}), bf16[3072,1024]{1,0:T(8,128)(2,1)}) %all-gather.17.cloned.1.call-update) | async-done | bytes 6291472 | tf_op jit(solution)/shard_map/all_gather | solution.py:32
  920.3 550.5 %while.28 = (s32[]{:T(128)}, f32[3072,4,64]{0,2,1:T(8,128)}, f32[3072,4,64]{0,2,1:T(8,128)S(1)}, bf16[6,512,4,64]{1,3,2,0:T(8,128)(2,1)}, s32[6]{0:T(128)S(1)}, ...) while((s32[]{:T(128)}, f32[3072,4,64]{0,2,1:T(8,128)}, ...), condition=%wide.region_15.16_spmd.clone, body=%wide.region_13.15_spmd.clone.sunk | while | flops 4099931136 | bytes 210566432 | solution.py:117
  928.0 13.4 fusion.155
  941.4 19.5 %multiply_reduce_fusion.12 = (f32[4,512]{1,0:T(4,128)S(1)}, f32[4,512,3072]{2,1,0:T(8,128)}) fusion(f32[4,512,3072]{2,1,0:T(8,128)} %fusion.155, f32[4,512]{1,0:T(4,128)S(1)} %dynamic-slice_bitcast_fusion.2, bf16[3072,4,64]{0,2,1:T(8,128)(2,1)} %get-tuple-element.525, bf16[3072,4,64]{0,2,1:T(8,128)(2,1)} %get-tuple-element.523, s32[]{:T(128)S(6)} %select_n.67, ...), kind=kOutput, calls=%fused_computation.19.clone.1 | convolution fusion | flops 843053056 | bytes 53755908 | tf_op jit(solution)/shard_map/while/body/eval_jaxpr/bhd,khd->hbk/dot_general | solution.py:56
  960.9 21.9 %multiply_convert_fusion.4 = bf16[4,512,3072]{2,1,0:T(8,128)(2,1)} fusion(f32[4,512,3072]{2,1,0:T(8,128)} %get-tuple-element.448, f32[4,512,3072]{2,1,0:T(8,128)} %fusion.155, f32[4,512]{1,0:T(4,128)S(1)} %get-tuple-element.449), kind=kLoop, calls=%fused_computation.18.clone.1 | loop fusion | flops 18874368 | bytes 62922752 | tf_op jit(solution)/shard_map/while/body/eval_jaxpr/convert_element_type | solution.py:96
  982.8 11.2 fusion.158
  994.1 9.9 fusion.159
  1020.3 14.0 fusion.155
  1034.3 19.5 %multiply_reduce_fusion.12 = (f32[4,512]{1,0:T(4,128)S(1)}, f32[4,512,3072]{2,1,0:T(8,128)}) fusion(f32[4,512,3072]{2,1,0:T(8,128)} %fusion.155, f32[4,512]{1,0:T(4,128)S(1)} %dynamic-slice_bitcast_fusion.2, bf16[3072,4,64]{0,2,1:T(8,128)(2,1)} %get-tuple-element.525, bf16[3072,4,64]{0,2,1:T(8,128)(2,1)} %get-tuple-element.523, s32[]{:T(128)S(6)} %select_n.67, ...), kind=kOutput, calls=%fused_computation.19.clone.1 | convolution fusion | flops 843053056 | bytes 53755908 | tf_op jit(solution)/shard_map/while/body/eval_jaxpr/bhd,khd->hbk/dot_general | solution.py:56
  1053.8 21.5 %multiply_convert_fusion.4 = bf16[4,512,3072]{2,1,0:T(8,128)(2,1)} fusion(f32[4,512,3072]{2,1,0:T(8,128)} %get-tuple-element.448, f32[4,512,3072]{2,1,0:T(8,128)} %fusion.155, f32[4,512]{1,0:T(4,128)S(1)} %get-tuple-element.449), kind=kLoop, calls=%fused_computation.18.clone.1 | loop fusion | flops 18874368 | bytes 62922752 | tf_op jit(solution)/shard_map/while/body/eval_jaxpr/convert_element_type | solution.py:96
  1075.3 11.0 fusion.158
  1112.7 13.3 fusion.155
  1125.9 19.4 %multiply_reduce_fusion.12 = (f32[4,512]{1,0:T(4,128)S(1)}, f32[4,512,3072]{2,1,0:T(8,128)}) fusion(f32[4,512,3072]{2,1,0:T(8,128)} %fusion.155, f32[4,512]{1,0:T(4,128)S(1)} %dynamic-slice_bitcast_fusion.2, bf16[3072,4,64]{0,2,1:T(8,128)(2,1)} %get-tuple-element.525, bf16[3072,4,64]{0,2,1:T(8,128)(2,1)} %get-tuple-element.523, s32[]{:T(128)S(6)} %select_n.67, ...), kind=kOutput, calls=%fused_computation.19.clone.1 | convolution fusion | flops 843053056 | bytes 53755908 | tf_op jit(solution)/shard_map/while/body/eval_jaxpr/bhd,khd->hbk/dot_general | solution.py:56
  1145.3 21.3 %multiply_convert_fusion.4 = bf16[4,512,3072]{2,1,0:T(8,128)(2,1)} fusion(f32[4,512,3072]{2,1,0:T(8,128)} %get-tuple-element.448, f32[4,512,3072]{2,1,0:T(8,128)} %fusion.155, f32[4,512]{1,0:T(4,128)S(1)} %get-tuple-element.449), kind=kLoop, calls=%fused_computation.18.clone.1 | loop fusion | flops 18874368 | bytes 62922752 | tf_op jit(solution)/shard_map/while/body/eval_jaxpr/convert_element_type | solution.py:96
  1166.6 11.0 fusion.158
  1204.0 13.3 fusion.155
  1217.2 19.4 %multiply_reduce_fusion.12 = (f32[4,512]{1,0:T(4,128)S(1)}, f32[4,512,3072]{2,1,0:T(8,128)}) fusion(f32[4,512,3072]{2,1,0:T(8,128)} %fusion.155, f32[4,512]{1,0:T(4,128)S(1)} %dynamic-slice_bitcast_fusion.2, bf16[3072,4,64]{0,2,1:T(8,128)(2,1)} %get-tuple-element.525, bf16[3072,4,64]{0,2,1:T(8,128)(2,1)} %get-tuple-element.523, s32[]{:T(128)S(6)} %select_n.67, ...), kind=kOutput, calls=%fused_computation.19.clone.1 | convolution fusion | flops 843053056 | bytes 53755908 | tf_op jit(solution)/shard_map/while/body/eval_jaxpr/bhd,khd->hbk/dot_general | solution.py:56
  1236.6 21.3 %multiply_convert_fusion.4 = bf16[4,512,3072]{2,1,0:T(8,128)(2,1)} fusion(f32[4,512,3072]{2,1,0:T(8,128)} %get-tuple-element.448, f32[4,512,3072]{2,1,0:T(8,128)} %fusion.155, f32[4,512]{1,0:T(4,128)S(1)} %get-tuple-element.449), kind=kLoop, calls=%fused_computation.18.clone.1 | loop fusion | flops 18874368 | bytes 62922752 | tf_op jit(solution)/shard_map/while/body/eval_jaxpr/convert_element_type | solution.py:96
  1257.9 11.0 fusion.158
  1268.9 9.6 fusion.159
  1295.3 13.3 fusion.155
  1308.6 19.4 %multiply_reduce_fusion.12 = (f32[4,512]{1,0:T(4,128)S(1)}, f32[4,512,3072]{2,1,0:T(8,128)}) fusion(f32[4,512,3072]{2,1,0:T(8,128)} %fusion.155, f32[4,512]{1,0:T(4,128)S(1)} %dynamic-slice_bitcast_fusion.2, bf16[3072,4,64]{0,2,1:T(8,128)(2,1)} %get-tuple-element.525, bf16[3072,4,64]{0,2,1:T(8,128)(2,1)} %get-tuple-element.523, s32[]{:T(128)S(6)} %select_n.67, ...), kind=kOutput, calls=%fused_computation.19.clone.1 | convolution fusion | flops 843053056 | bytes 53755908 | tf_op jit(solution)/shard_map/while/body/eval_jaxpr/bhd,khd->hbk/dot_general | solution.py:56
  1327.9 21.3 %multiply_convert_fusion.4 = bf16[4,512,3072]{2,1,0:T(8,128)(2,1)} fusion(f32[4,512,3072]{2,1,0:T(8,128)} %get-tuple-element.448, f32[4,512,3072]{2,1,0:T(8,128)} %fusion.155, f32[4,512]{1,0:T(4,128)S(1)} %get-tuple-element.449), kind=kLoop, calls=%fused_computation.18.clone.1 | loop fusion | flops 18874368 | bytes 62922752 | tf_op jit(solution)/shard_map/while/body/eval_jaxpr/convert_element_type | solution.py:96
  1349.2 11.0 fusion.158
  1360.2 9.6 fusion.159
  1386.6 13.3 fusion.155
  1399.9 19.4 %multiply_reduce_fusion.12 = (f32[4,512]{1,0:T(4,128)S(1)}, f32[4,512,3072]{2,1,0:T(8,128)}) fusion(f32[4,512,3072]{2,1,0:T(8,128)} %fusion.155, f32[4,512]{1,0:T(4,128)S(1)} %dynamic-slice_bitcast_fusion.2, bf16[3072,4,64]{0,2,1:T(8,128)(2,1)} %get-tuple-element.525, bf16[3072,4,64]{0,2,1:T(8,128)(2,1)} %get-tuple-element.523, s32[]{:T(128)S(6)} %select_n.67, ...), kind=kOutput, calls=%fused_computation.19.clone.1 | convolution fusion | flops 843053056 | bytes 53755908 | tf_op jit(solution)/shard_map/while/body/eval_jaxpr/bhd,khd->hbk/dot_general | solution.py:56
  1419.3 21.3 %multiply_convert_fusion.4 = bf16[4,512,3072]{2,1,0:T(8,128)(2,1)} fusion(f32[4,512,3072]{2,1,0:T(8,128)} %get-tuple-element.448, f32[4,512,3072]{2,1,0:T(8,128)} %fusion.155, f32[4,512]{1,0:T(4,128)S(1)} %get-tuple-element.449), kind=kLoop, calls=%fused_computation.18.clone.1 | loop fusion | flops 18874368 | bytes 62922752 | tf_op jit(solution)/shard_map/while/body/eval_jaxpr/convert_element_type | solution.py:96
  1440.6 11.0 fusion.158
  1451.5 9.6 fusion.159
  1533.2 61.9 %reduce-scatter.15.cloned.1.call-done = f32[4,128,256]{1,2,0:T(8,128)} async-done(((f32[4,1024,256]{1,2,0:T(8,128)}), f32[4,128,256]{1,2,0:T(8,128)}) %reduce-scatter.15.cloned.1.call-update) | async-done | bytes 524304 | tf_op jit(solution)/shard_map/reduce_scatter | solution.py:279
  1604.7 92.1 %reduce-scatter.13.cloned.1.call-done = f32[768,1024]{1,0:T(8,128)} async-done(((f32[3072,1024]{1,0:T(8,128)}), f32[768,1024]{1,0:T(8,128)}) %reduce-scatter.13.cloned.1.call-update) | async-done | bytes 3145744 | tf_op jit(solution)/shard_map/reduce_scatter | solution.py:36
  1701.7 40.4 %all-reduce = (f32[6]{0:T(128)S(1)}, f32[6]{0:T(128)S(1)}, f32[14,1024]{1,0:T(8,128)}, f32[5]{0:T(128)S(1)}) all-reduce(f32[6]{0:T(128)S(1)} %get-tuple-element.317, f32[6]{0:T(128)S(1)} %get-tuple-element.316, f32[14,1024]{1,0:T(8,128)S(1)} %concatenate.15, f32[5]{0:T(128)S(1)} %copy-done.69), channel_id=1, replica_groups=mesh['dp'=8,'tensor'=4] {'dp','tensor'}, use_global_device_ids=true, to_apply=%region_26.27 | all-reduce | flops 14353 | bytes 114824 | tf_op jit(solution)/shard_map/psum | solution.py:294
  (332 shorter events, 295.0 us)
Async XLA Ops:
  7.2 2.3 copy-start.2
  7.2 3.8 copy-start.30
  7.2 56.5 %all-gather.9.cloned.1.call-start = ((), (), s32[]{:S(2)}) async-start(), calls=%async_computation.7 | async-start | bytes 2359296 | tf_op jit(solution)/shard_map/all_gather | solution.py:155
  8.6 5.3 copy-start.16
  9.4 101.0 %all-gather.7.cloned.1.call-start = ((), (), s32[]{:S(2)}) async-start(), calls=%async_computation.6 | async-start | bytes 7864320 | tf_op jit(solution)/shard_map/all_gather | solution.py:32
  14.0 463.7 %reduce-scatter.7.cloned.1.call-start = ((), (), s32[]{:S(2)}) async-start(), calls=%async_computation.8 | async-start | bytes 15728640 | tf_op jit(solution)/shard_map/reduce_scatter | solution.py:36
  365.2 4.2 copy-start.5
  365.2 4.2 copy-start.20
  377.9 99.8 %copy-start.50 = (f32[1,1024]{1,0:T(1,128)S(1)}, f32[1,1024]{1,0:T(1,128)}, u32[]{:S(2)}) copy-start(f32[1,1024]{1,0:T(1,128)} %get-tuple-element.303) | copy-start | bytes 12292
  377.9 99.8 %copy-start.52 = (f32[1,1024]{1,0:T(1,128)S(1)}, f32[1,1024]{1,0:T(1,128)}, u32[]{:S(2)}) copy-start(f32[1,1024]{1,0:T(1,128)} %get-tuple-element.304) | copy-start | bytes 12292
  377.9 99.8 %copy-start.3 = (bf16[768,1024]{1,0:T(8,128)(2,1)S(1)}, bf16[768,1024]{1,0:T(8,128)(2,1)}, u32[]{:S(2)}) copy-start(bf16[768,1024]{1,0:T(8,128)(2,1)} %param.16) | copy-start | bytes 4718596
  378.0 175.1 %all-gather.13.cloned.1.call-start = ((), (), s32[]{:S(2)}) async-start(), calls=%async_computation.10 | async-start | bytes 4718592 | tf_op jit(solution)/shard_map/all_gather | solution.py:156
  380.0 220.0 %all-gather.11.cloned.1.call-start = ((), (), s32[]{:S(2)}) async-start(), calls=%async_computation.9 | async-start | bytes 7864320 | tf_op jit(solution)/shard_map/all_gather | solution.py:32
  480.2 3.4 copy-start.39
  480.7 2.9 copy-start.45
  481.9 2.5 copy-start.9
  481.9 2.5 copy-start.54
  483.6 165.5 %all-gather.15.cloned.1.call-start = ((), (), s32[]{:S(2)}) async-start(), calls=%async_computation.12 | async-start | bytes 7864320 | tf_op jit(solution)/shard_map/all_gather | solution.py:32
  484.3 152.9 %copy-start.36 = (f32[768]{0:T(1024)}, f32[768]{0:T(1024)S(1)}, u32[]{:S(2)}) copy-start(f32[768]{0:T(1024)S(1)} %get-tuple-element.277) | copy-start | bytes 9220
  485.9 264.1 %reduce-scatter.9.cloned.1.call-start = ((), (), s32[]{:S(2)}) async-start(), calls=%async_computation.11 | async-start | bytes 15728640 | tf_op jit(solution)/shard_map/reduce_scatter | solution.py:36
  600.0 39.9 %copy-start.70 = (bf16[2,1024,1024]{2,1,0:T(8,128)(2,1)S(1)}, bf16[2,1024,1024]{2,1,0:T(8,128)(2,1)}, u32[]{:S(2)}) copy-start(bf16[2,1024,1024]{2,1,0:T(8,128)(2,1)} %all-gather.13.cloned.1.call-done) | copy-start | bytes 12582916
  637.2 2.6 copy-start.72
  649.0 203.3 %reduce-scatter.11.cloned.1.call-start = ((), (), s32[]{:S(2)}) async-start(), calls=%async_computation.13 | async-start | bytes 15728640 | tf_op jit(solution)/shard_map/reduce_scatter | solution.py:36
  649.1 24.6 %copy-start.71 = (bf16[2,1024,1024]{2,1,0:T(8,128)(2,1)S(1)}, bf16[2,1024,1024]{2,1,0:T(8,128)(2,1)}, u32[]{:S(2)}) copy-start(bf16[2,1024,1024]{2,1,0:T(8,128)(2,1)} %all-gather.13.cloned.1.call-done) | copy-start | bytes 12582916
  686.1 166.1 %copy-start.1 = (f32[768,1024]{1,0:T(8,128)S(1)}, f32[768,1024]{1,0:T(8,128)}, u32[]{:S(2)}) copy-start(f32[768,1024]{1,0:T(8,128)} %copy-done) | copy-start | bytes 9437188
  686.1 166.1 %copy-start.37 = (f32[768]{0:T(1024)S(1)}, f32[768]{0:T(1024)}, u32[]{:S(2)}) copy-start(f32[768]{0:T(1024)} %copy-done.36) | copy-start | bytes 9220
  686.1 166.1 %copy-start.40 = (f32[768]{0:T(1024)S(1)}, f32[768]{0:T(1024)}, u32[]{:S(2)}) copy-start(f32[768]{0:T(1024)} %copy-done.39) | copy-start | bytes 9220
  686.1 166.1 %copy-start.44 = (f32[1,1024]{1,0:T(1,128)S(1)}, f32[1,1024]{1,0:T(1,128)}, u32[]{:S(2)}) copy-start(f32[1,1024]{1,0:T(1,128)} %get-tuple-element.302) | copy-start | bytes 12292
  686.2 166.1 %copy-start.46 = (f32[768]{0:T(1024)S(1)}, f32[768]{0:T(1024)}, u32[]{:S(2)}) copy-start(f32[768]{0:T(1024)} %copy-done.45) | copy-start | bytes 9220
  686.2 166.1 %copy-start.55 = (f32[1,1024]{1,0:T(1,128)S(1)}, f32[1,1024]{1,0:T(1,128)}, u32[]{:S(2)}) copy-start(f32[1,1024]{1,0:T(1,128)} %get-tuple-element.307) | copy-start | bytes 12292
  686.2 166.1 %copy-start.64 = (f32[1,1024]{1,0:T(1,128)S(1)}, f32[1,1024]{1,0:T(1,128)}, u32[]{:S(2)}) copy-start(f32[1,1024]{1,0:T(1,128)} %get-tuple-element.300) | copy-start | bytes 12292
  686.2 228.1 %all-gather.17.cloned.1.call-start = ((), (), s32[]{:S(2)}) async-start(), calls=%async_computation.14 | async-start | bytes 7864320 | tf_op jit(solution)/shard_map/all_gather | solution.py:32
  852.3 8.6 copy-start.59
  852.3 8.6 copy-start.13
  860.9 3.2 copy-start.12
  860.9 3.2 copy-start.51
  860.9 3.1 copy-start.53
  862.0 5.8 copy-start.8
  862.0 5.8 copy-start.48
  867.8 655.2 %reduce-scatter.17.cloned.1.call-start = ((), (), s32[]{:S(2)}) async-start(), calls=%async_computation.17 | async-start | bytes 9437184 | tf_op jit(solution)/shard_map/reduce_scatter | solution.py:280
  893.5 26.8 %copy-start.23 = (s32[3072]{0:T(1024)S(1)}, s32[3072]{0:T(1024)}, u32[]{:S(2)}) copy-start(s32[3072]{0:T(1024)} %param.18) | copy-start | bytes 36868
  893.5 701.6 %reduce-scatter.15.cloned.1.call-start = ((), (), s32[]{:S(2)}) async-start(), calls=%async_computation.16 | async-start | bytes 4718592 | tf_op jit(solution)/shard_map/reduce_scatter | solution.py:279
  1489.2 2.8 copy-start.19
  1492.0 4.7 copy-start.24
  1492.0 4.8 copy-start.25
  1492.0 4.8 copy-start.27
  1506.5 190.2 %reduce-scatter.13.cloned.1.call-start = ((), (), s32[]{:S(2)}) async-start(), calls=%async_computation.15 | async-start | bytes 15728640 | tf_op jit(solution)/shard_map/reduce_scatter | solution.py:36
  1517.4 4.1 copy-start.21
  1517.4 4.7 copy-start.68
  1518.5 4.5 copy-start.15
  1518.5 4.5 copy-start.28
  1523.0 72.1 %copy-start.17 = (f32[4,128,256]{1,2,0:T(8,128)S(1)}, f32[4,128,256]{1,2,0:T(8,128)}, u32[]{:S(2)}) copy-start(f32[4,128,256]{1,2,0:T(8,128)} %copy-done.16) | copy-start | bytes 1572868
  1533.1 163.6 %copy-start.4 = (bf16[768,1024]{1,0:T(8,128)(2,1)S(1)}, bf16[768,1024]{1,0:T(8,128)(2,1)}, u32[]{:S(2)}) copy-start(bf16[768,1024]{1,0:T(8,128)(2,1)} %param.16) | copy-start | bytes 4718596
  1533.2 163.6 %copy-start.33 = (f32[768]{0:T(1024)S(1)}, f32[768]{0:T(1024)}, u32[]{:S(2)}) copy-start(f32[768]{0:T(1024)} %copy-done.32) | copy-start | bytes 9220
  1533.2 163.6 %copy-start.35 = (f32[1,1024]{1,0:T(1,128)S(1)}, f32[1,1024]{1,0:T(1,128)}, u32[]{:S(2)}) copy-start(f32[1,1024]{1,0:T(1,128)} %copy-done.34) | copy-start | bytes 12292
  1601.7 98.0 %copy-start.57 = (f32[768]{0:T(1024)S(1)}, f32[768]{0:T(1024)}, u32[]{:S(2)}) copy-start(f32[768]{0:T(1024)} %copy-done.56) | copy-start | bytes 9220
  1601.7 98.0 %copy-start.42 = (f32[768]{0:T(1024)S(1)}, f32[768]{0:T(1024)}, u32[]{:S(2)}) copy-start(f32[768]{0:T(1024)} %copy-done.41) | copy-start | bytes 9220
  1696.8 2.9 copy-start.6
  1699.7 2.0 copy-start.69
  1701.5 46.0 %copy-start.31 = (f32[14,1024]{1,0:T(8,128)S(1)}, f32[14,1024]{1,0:T(8,128)}, u32[]{:S(2)}) copy-start(f32[14,1024]{1,0:T(8,128)} %param.25) | copy-start | bytes 172036
  1744.8 8.2 copy-start.11
  1744.8 8.2 copy-start.38
  1744.8 8.2 copy-start.49
  1746.9 6.1 copy-start.7
  (21 other events, 30.3 us)
Sparse Core Ops, SparseCore 0:
  10.6 53.0 all-gather.8
  65.9 44.5 all-gather.6
  378.1 99.5 reduce-scatter.6
  480.3 72.7 all-gather.12
  555.1 44.8 all-gather.10
  601.4 46.3 all-gather.14
  650.4 99.5 reduce-scatter.8
  752.6 99.6 reduce-scatter.10
  868.0 46.3 all-gather.16
  918.4 147.4 reduce-scatter.16
  1506.7 88.3 reduce-scatter.14
  1597.5 99.2 reduce-scatter.12
where the time goes:
time: 1780 us; the launch traced here: 1760 us
  matrix products  673 us (38%)
  waiting for transfers between devices  648 us (36%)
  other arithmetic  301 us (17%)
  local copies, waits for them, and re-layouts  65.7 us (4%)
  blocking collectives  40.4 us (2%)
  loops' own time  20.5 us (1%)
    reduce_scatter x4, waiting for transfers between devices, sum_product(): lax.psum_scatter(jnp.einsum('sgk,sdk->gd', left_operand, right_operand, p...  356 us
    dot_general x12, matrix products, block_scores(): jnp.einsum('bhd,khd->hbk', block_query, key_heads, preferred_element_type...  190 us
    convert_element_type x6, other arithmetic, one_block(): grad_scores = (soft * (grad_soft - inner)).astype(jnp.bfloat16)  129 us
    all_gather x4, waiting for transfers between devices, gather_rows(): return lax.all_gather(values, 'tensor', axis=0, tiled=True)  114 us
    dot_general x6, matrix products, one_block(): jnp.einsum('bhd,khd->hbk', block_grad, value_heads, preferred_element_typ...  80.5 us
    dot_general x6, matrix products, one_block(): jnp.einsum('hbk,khd->bhd', probs, value_heads, preferred_element_type=jnp...  73.9 us
    reduce_sum x6, other arithmetic, one_block(): totals = jnp.sum(raised, axis=-1, keepdims=True)  71.3 us
    all_gather x1, waiting for transfers between devices, per_device(): lax.all_gather(mlp_master.astype(jnp.bfloat16), 'dp', axis=1, tiled=True)  66.3 us
  transfers between devices with their start and end apart: 12, of which 10 were waited for; matrix products, arithmetic and copies ran while one was open for 41% of the time, Pallas kernels for 0%

commit v1 on v0

v1 whole, which is shorter than its diff:
```python
import functools

import jax
import jax.numpy as jnp
from jax import lax
from jax.experimental import pallas as pl
from jax.experimental.pallas import tpu as pltpu
from jax.sharding import Mesh
from jax.sharding import PartitionSpec as P

HEAD_DIM = 64
IMAGE = 1370
STEP = 3
LANES = 128
QROWS = 352
ROW_TILE = 16
MESH = pl.DeviceIdType.MESH


beta_rate = 0.5
adam_epsilon = 1e-06
norm_epsilon = 1e-06
learning_rate = 0.5
vector_rate = 0.05
weight_decay = 0.05
masked_score = -1e30

DEVICES = ("z", "x", "y", "core")
CHIPS = ("z", "x", "y")
SWAP = ((0, 1), (1, 0))
NT = (((1,), (1,)), ((), ()))
bf16 = jnp.bfloat16
f32 = jnp.float32


def round_up(value, step):
    return -(-value // step) * step


def low_lanes():
    return lax.broadcasted_iota(jnp.int32, (QROWS, LANES), 1) < HEAD_DIM


def inside(place, limits):
    return (place < limits[0]) | ((place >= limits[1]) & (place < limits[2]))


def key_bias(limits, rows):
    place = lax.broadcasted_iota(jnp.int32, (1, rows), 1)
    return jnp.where(inside(place, limits), 0.0, masked_score)


def masked_scores(query, keys, bias):
    return lax.dot_general(query, keys, NT, preferred_element_type=f32) + bias


def attend_forward_kernel(limit_ref, q_ref, k_ref, v_ref, own_ref, out_ref, logsum_ref):
    low = low_lanes()
    query = q_ref[...] * jnp.asarray(HEAD_DIM ** (-0.5), bf16)
    keys = k_ref[...]
    values = v_ref[...]
    limits = [limit_ref[i] for i in range(3)]
    bias = key_bias(limits, keys.shape[0])
    outputs = []
    logsums = []
    for half in range(2):
        own = low if half == 0 else ~low
        scores = masked_scores(jnp.where(own, query, jnp.zeros_like(query)), keys, bias)
        largest = jnp.max(scores, axis=1, keepdims=True)
        raised = jnp.exp(scores - largest)
        totals = jnp.sum(raised, axis=1, keepdims=True)
        probs = (raised * (1.0 / totals)).astype(bf16)
        outputs.append(jnp.dot(probs, values, preferred_element_type=f32))
        logsums.append(largest + jnp.log(totals))
    row = pl.program_id(1) * QROWS + lax.broadcasted_iota(jnp.int32, (QROWS, LANES), 0)
    mixed = jnp.where(low, outputs[0], outputs[1])
    mixed = jnp.where(inside(row, limits), mixed, own_ref[...].astype(f32))
    out_ref[...] = mixed.astype(bf16)
    logsum_ref[...] = jnp.where(low, logsums[0], logsums[1])


def attend_forward(limit, query, keys, values, rows):
    pairs = query.shape[1] // LANES
    flops = 4 * 2 * pairs * rows * rows * LANES
    return pl.pallas_call(
        attend_forward_kernel,
        grid_spec=pltpu.PrefetchScalarGridSpec(
            num_scalar_prefetch=1,
            grid=(pairs, rows // QROWS),
            in_specs=[
                pl.BlockSpec((QROWS, LANES), lambda p, i, s: (i, p)),
                pl.BlockSpec((rows, LANES), lambda p, i, s: (0, p)),
                pl.BlockSpec((rows, LANES), lambda p, i, s: (0, p)),
                pl.BlockSpec((QROWS, LANES), lambda p, i, s: (i, p)),
            ],
            out_specs=[
                pl.BlockSpec((QROWS, LANES), lambda p, i, s: (i, p)),
                pl.BlockSpec((QROWS, LANES), lambda p, i, s: (i, p)),
            ],
        ),
        out_shape=(
            jax.ShapeDtypeStruct((rows, pairs * LANES), bf16),
            jax.ShapeDtypeStruct((rows, pairs * LANES), f32),
        ),
        compiler_params=pltpu.CompilerParams(vmem_limit_bytes=48 << 20),
        cost_estimate=pl.CostEstimate(
            flops=flops, bytes_accessed=8 * rows * pairs * LANES, transcendentals=2 * pairs * rows * rows
        ),
        name="attend_forward",
    )(limit, query, keys, values, values)


def attend_backward_kernel(
    limit_ref, q_ref, k_ref, v_ref, grad_ref, logsum_ref, dq_ref, dk_ref, dv_ref, keys_acc, values_acc
):
    step = pl.program_id(1)
    low = low_lanes()
    scale = jnp.asarray(HEAD_DIM ** (-0.5), bf16)
    query = q_ref[...] * scale
    keys = k_ref[...]
    values = v_ref[...]
    grads = grad_ref[...]
    bias = key_bias([limit_ref[i] for i in range(3)], keys.shape[0])

    @pl.when(step == 0)
    def _():
        keys_acc[...] = jnp.zeros_like(keys_acc)
        values_acc[...] = jnp.zeros_like(values_acc)

    outputs = []
    for half in range(2):
        own = low if half == 0 else ~low
        head_query = jnp.where(own, query, jnp.zeros_like(query))
        head_grads = jnp.where(own, grads, jnp.zeros_like(grads))
        logsum = logsum_ref[:, half * HEAD_DIM : half * HEAD_DIM + 1]
        soft = jnp.exp(masked_scores(head_query, keys, bias) - logsum)
        grad_soft = lax.dot_general(head_grads, values, NT, preferred_element_type=f32)
        inner = jnp.sum(soft * grad_soft, axis=1, keepdims=True)
        grad_scores = (soft * (grad_soft - inner)).astype(bf16)
        outputs.append(jnp.dot(grad_scores, keys, preferred_element_type=f32))
        keys_acc[...] += jnp.dot(head_query.T, grad_scores, preferred_element_type=f32)
        values_acc[...] += jnp.dot(head_grads.T, soft.astype(bf16), preferred_element_type=f32)
    dq_ref[...] = (jnp.where(low, outputs[0], outputs[1]) * HEAD_DIM ** (-0.5)).astype(bf16)

    @pl.when(step == pl.num_programs(1) - 1)
    def _():
        dk_ref[...] = keys_acc[...].astype(bf16).T
        dv_ref[...] = values_acc[...].astype(bf16).T


def attend_backward(limit, query, keys, values, grad_mixed, logsum):
    rows, columns = grad_mixed.shape
    pairs = columns // LANES
    flops = 10 * 2 * pairs * rows * rows * LANES
    shape = jax.ShapeDtypeStruct((rows, columns), bf16)
    return pl.pallas_call(
        attend_backward_kernel,
        grid_spec=pltpu.PrefetchScalarGridSpec(
            num_scalar_prefetch=1,
            grid=(pairs, rows // QROWS),
            in_specs=[
                pl.BlockSpec((QROWS, LANES), lambda p, i, s: (i, p)),
                pl.BlockSpec((rows, LANES), lambda p, i, s: (0, p)),
                pl.BlockSpec((rows, LANES), lambda p, i, s: (0, p)),
                pl.BlockSpec((QROWS, LANES), lambda p, i, s: (i, p)),
                pl.BlockSpec((QROWS, LANES), lambda p, i, s: (i, p)),
            ],
            out_specs=[
                pl.BlockSpec((QROWS, LANES), lambda p, i, s: (i, p)),
                pl.BlockSpec((rows, LANES), lambda p, i, s: (0, p)),
                pl.BlockSpec((rows, LANES), lambda p, i, s: (0, p)),
            ],
            scratch_shapes=[pltpu.VMEM((LANES, rows), f32), pltpu.VMEM((LANES, rows), f32)],
        ),
        out_shape=(shape, shape, shape),
        compiler_params=pltpu.CompilerParams(vmem_limit_bytes=48 << 20),
        cost_estimate=pl.CostEstimate(
            flops=flops, bytes_accessed=16 * rows * columns, transcendentals=2 * pairs * rows * rows
        ),
        name="attend_backward",
    )(limit, query, keys, values, grad_mixed, logsum)


def norm_parts(values):
    average = jnp.mean(values, axis=-1, keepdims=True)
    centered = values - average
    variance = jnp.mean(centered * centered, axis=-1, keepdims=True)
    inverse = lax.rsqrt(variance + norm_epsilon)
    return (centered * inverse, inverse)


def norm_back(unit, inverse, gain, grads):
    scaled = grads * gain
    first = jnp.mean(scaled, axis=-1, keepdims=True)
    second = jnp.mean(scaled * unit, axis=-1, keepdims=True)
    return inverse * (scaled - first - unit * second)


def adapt_moments(gradient, first, second):
    new_first = beta_rate * first + (1.0 - beta_rate) * gradient
    new_second = beta_rate * second + (1.0 - beta_rate) * gradient * gradient
    first_hat = new_first / (1.0 - beta_rate**STEP)
    second_hat = new_second / (1.0 - beta_rate**STEP)
    return (new_first, new_second, first_hat / (jnp.sqrt(second_hat) + adam_epsilon))


def swap_cores(values):
    return lax.ppermute(values, "core", SWAP)


def sum_cores(partial):
    sent = partial.astype(bf16)
    return sent.astype(f32) + swap_cores(sent).astype(f32)


def gather_weights(shard):
    blocks = lax.all_gather(shard, CHIPS, axis=0, tiled=False)
    outer = blocks.shape[0] // 2
    count, depth, columns = shard.shape
    blocks = blocks.reshape(outer, 2, count, depth, columns).transpose(2, 0, 3, 1, 4)
    return blocks.reshape(count, outer * depth, 2 * columns)


def scatter_grads(grads, depth, columns):
    count = grads.shape[0]
    outer = grads.shape[1] // depth
    blocks = grads.reshape(count, outer, depth, 2, columns).transpose(1, 3, 0, 2, 4)
    blocks = blocks.reshape(outer * 2, count, depth, columns)
    return lax.psum_scatter(blocks, CHIPS, scatter_dimension=0, tiled=False)


def neighbour(axis, shift):
    size = lax.axis_size(axis)
    return lax.rem(lax.axis_index(axis) + shift + size, size)


def row_plan(local_rows):
    chip_rows = 2 * local_rows
    extra = chip_rows - IMAGE
    lent = round_up(extra, ROW_TILE)
    head = round_up(IMAGE - extra, ROW_TILE)
    return (chip_rows, extra, lent, head, chip_rows + lent, round_up(head + lent, LANES))


def exchange_kernel(
    with_weights, tokens_ref, cotangent_ref, attn_ref, mlp_ref, *outs_and_scratch
):
    count = 8 if with_weights else 2
    outs = outs_and_scratch[:count]
    row_local, row_send, row_recv, own_sem, send_sem, recv_sem = outs_and_scratch[count:]
    depth = lax.axis_size("z")
    z, x, y, core = (lax.axis_index(axis) for axis in DEVICES)
    up, down = neighbour("z", 1), neighbour("z", -1)
    other_x, other_y, other_core = 1 - x, 1 - y, 1 - core

    barrier = pltpu.get_barrier_semaphore()
    greeted = [{"core": other_core}, {"y": other_y}, {"y": other_y, "core": other_core}]
    if with_weights:
        greeted += [{"z": up}, {"z": down}, {"x": other_x}]
    for device in greeted:
        pl.semaphore_signal(barrier, inc=1, device_id=device, device_id_type=MESH)
    pl.semaphore_wait(barrier, len(greeted))

    local_rows = tokens_ref.shape[0]
    chip_rows, extra, lent, head, rows, live = row_plan(local_rows)
    split = head - local_rows
    first = pl.multiple_of(core * local_rows, ROW_TILE)
    second = pl.multiple_of(core * local_rows + split + core * y * lent, ROW_TILE)
    lent_place = pl.multiple_of(y * chip_rows + (1 - y) * head, ROW_TILE)
    spans = [(0, split, first), (split, local_rows - split, second)]

    def remote(source, target, send, recv, device):
        return pltpu.make_async_remote_copy(
            src_ref=source,
            dst_ref=target,
            send_sem=send,
            recv_sem=recv,
            device_id=device,
            device_id_type=MESH,
        )

    def lend(array, source, target, to_core):
        return remote(
            source.at[pl.ds(local_rows - lent, lent)],
            target.at[pl.ds(lent_place, lent)],
            row_send.at[array, 2 + to_core],
            row_recv.at[array, 2],
            {"y": other_y, "core": to_core},
        )

    row_copies = []
    for array, source in enumerate((tokens_ref, cotangent_ref)):
        target = outs[array]
        for part, (begin, size, place) in enumerate(spans):
            window = target.at[pl.ds(place, size)]
            row_copies.append(
                (
                    pltpu.make_async_copy(
                        source.at[pl.ds(begin, size)], window, row_local.at[array, part]
                    ),
                    remote(
                        source.at[pl.ds(begin, size)],
                        window,
                        row_send.at[array, part],
                        row_recv.at[array, part],
                        {"core": other_core},
                    ),
                )
            )

    def start_rows():
        for local, shared in row_copies:
            shared.start()
            local.start()

        @pl.when(core == 1)
        def _():
            for array, source in enumerate((tokens_ref, cotangent_ref)):
                for to_core in range(2):
                    lend(array, source, outs[array], to_core).start()

    def finish_rows():
        for local, shared in row_copies:
            local.wait()
            shared.wait()
        for array, source in enumerate((tokens_ref, cotangent_ref)):
            lend(array, source, outs[array], 0).wait_recv()

        @pl.when(core == 1)
        def _():
            for array, source in enumerate((tokens_ref, cotangent_ref)):
                for to_core in range(2):
                    lend(array, source, outs[array], to_core).wait_send()

    if not with_weights:
        start_rows()
        finish_rows()
        return

    weights = []
    for index in range(6):
        source = attn_ref.at[index] if index < 4 else mlp_ref.at[index - 4]
        weights.append((index, source, outs[2 + index], source.shape[1]))

    def window(item, slot):
        index, source, target, columns = item
        return target.at[slot, x, :, pl.ds(pl.multiple_of(y * columns, LANES), columns)]

    def slot_of(step):
        return lax.rem(z - step + depth, depth)

    def local(item):
        return pltpu.make_async_copy(item[1], window(item, z), own_sem.at[item[0]])

    def ring(item, step):
        slot = slot_of(step - 1)
        source = item[1] if step == 1 else window(item, slot)
        place = step - 1
        return remote(
            source,
            window(item, slot),
            send_sem.at[item[0], place],
            recv_sem.at[item[0], place],
            {"z": up},
        )

    def by_x(item):
        return (item[0] % 2) == 0

    def cross(item, step):
        slot = slot_of(step)
        source = item[1] if step == 0 else window(item, slot)
        place = depth - 1 + step
        return remote(
            source,
            window(item, slot),
            send_sem.at[item[0], place],
            recv_sem.at[item[0], place],
            {"x": other_x} if by_x(item) else {"y": other_y},
        )

    def spread(item, step):
        index, source, target, columns = item
        slot = slot_of(step)
        if by_x(item):
            part = target.at[slot, :, :, pl.ds(pl.multiple_of(y * columns, LANES), columns)]
        else:
            part = target.at[slot, x]
        place = 2 * depth - 1 + step
        return remote(
            part,
            part,
            send_sem.at[index, place],
            recv_sem.at[index, place],
            {"y": other_y} if by_x(item) else {"x": other_x},
        )

    attn, mlp = weights[:4], weights[4:]
    for item in attn:
        ring(item, 1).start()
    for item in attn:
        cross(item, 0).start()
    for item in weights:
        local(item).start()
    start_rows()
    for item in weights:
        local(item).wait()

    def run(items, started, trailing):
        for step in range(depth):
            if step > 0:
                for item in items:
                    ring(item, step).wait_recv()
            if step + 1 < depth and (step > 0 or not started):
                for item in items:
                    ring(item, step + 1).start()
            if step == depth - 1:
                for item in trailing:
                    ring(item, 1).start()
            if step > 0 or not started:
                for item in items:
                    cross(item, step).start()
            if step > 0:
                for item in items:
                    cross(item, step - 1).wait_recv()
                    spread(item, step - 1).start()
        for item in items:
            cross(item, depth - 1).wait_recv()
            spread(item, depth - 1).start()

    def run_mlp():
        for item in mlp:
            cross(item, 0).start()
        run(mlp, True, [])

    run(attn, True, mlp)
    run_mlp()
    for item in weights:
        for step in range(depth):
            spread(item, step).wait()
            cross(item, step).wait_send()
            if step > 0:
                ring(item, step).wait_send()
    finish_rows()


def exchange(tokens, cotangent, attn_low, mlp_low, with_weights):
    local_rows, width = tokens.shape
    rows = row_plan(local_rows)[4]
    depth = lax.axis_size("z")
    shapes = [jax.ShapeDtypeStruct((rows, width), bf16)] * 2
    if with_weights:
        for weights in (attn_low, mlp_low):
            count, block, columns = weights.shape
            shapes += [jax.ShapeDtypeStruct((depth, 2, block, 2 * columns), bf16)] * count
    vmem = pl.BlockSpec(memory_space=pltpu.VMEM)
    places = 3 * depth - 1 if with_weights else 1
    outs = pl.pallas_call(
        functools.partial(exchange_kernel, with_weights),
        in_specs=[vmem] * 4,
        out_specs=[pl.BlockSpec(memory_space=pl.ANY)] * len(shapes),
        out_shape=shapes,
        scratch_shapes=[
            pltpu.SemaphoreType.DMA((2, 2)),
            pltpu.SemaphoreType.DMA((2, 4)),
            pltpu.SemaphoreType.DMA((2, 3)),
            pltpu.SemaphoreType.DMA((6,)),
            pltpu.SemaphoreType.DMA((6, places)),
            pltpu.SemaphoreType.DMA((6, places)),
        ],
        compiler_params=pltpu.CompilerParams(collective_id=0, has_side_effects=True),
        name="exchange",
    )(tokens, cotangent, attn_low, mlp_low)
    if with_weights:
        weights = [w.reshape(-1, w.shape[-1]) for w in outs[2:]]
    else:
        weights = list(gather_weights(attn_low)) + list(gather_weights(mlp_low))
    return (outs[0], outs[1], weights)


def scatter_short(grads, columns, by_x):
    depth = lax.axis_size("z")
    z, x, y, _ = (lax.axis_index(axis) for axis in DEVICES)
    block = grads.shape[0] // (2 * depth)

    def trade_y(values):
        sent = lax.dynamic_slice_in_dim(values, (1 - y) * columns, columns, values.ndim - 1)
        kept = lax.dynamic_slice_in_dim(values, y * columns, columns, values.ndim - 1)
        return kept.astype(f32) + lax.ppermute(sent.astype(bf16), "y", SWAP).astype(f32)

    def trade_x(values):
        sent = lax.dynamic_index_in_dim(values, 1 - x, 1, False)
        kept = lax.dynamic_index_in_dim(values, x, 1, False)
        return kept.astype(f32) + lax.ppermute(sent.astype(bf16), "x", SWAP).astype(f32)

    blocks = grads.reshape(depth, 2, block, 2 * columns)
    blocks = trade_y(trade_x(blocks)) if by_x else trade_x(trade_y(blocks))
    ring = tuple((i, (i + 1) % depth) for i in range(depth))
    moving = lax.dynamic_index_in_dim(blocks, lax.rem(z - 1 + depth, depth), 0, False)
    for step in range(1, depth):
        moving = lax.ppermute(moving.astype(bf16), "z", ring).astype(f32)
        place = lax.rem(z - 1 - step + 2 * depth, depth)
        moving = moving + lax.dynamic_index_in_dim(blocks, place, 0, False)
    return moving


def scatter_all(grads, depth, columns):
    if lax.axis_size("z") > 4:
        return scatter_grads(jnp.stack(grads), depth, columns)
    return jnp.stack([scatter_short(g, columns, i % 2 == 0) for i, g in enumerate(grads)])


def per_device(
    tokens,
    cotangent,
    image_ids,
    attn_master,
    attn_first,
    attn_second,
    mlp_master,
    mlp_first,
    mlp_second,
    vectors,
    vector_first,
    vector_second,
):
    local_rows, width = tokens.shape
    chip_rows, extra, lent, head, rows, live = row_plan(local_rows)
    core = lax.axis_index("core")
    upper_chip = lax.axis_index("y") == 1
    first_core = (core == 0).astype(f32)
    head_part = attn_master.shape[2]
    hidden_part = mlp_master.shape[2]

    attn_low = attn_master.astype(bf16)
    mlp_low = mlp_master.astype(bf16)
    arranged, seeds, weights = exchange(
        tokens, cotangent, attn_low, mlp_low, lax.axis_size("z") <= 4
    )
    query_full, key_full, value_full, out_full, up_full, down_full = weights

    image_live = lax.dynamic_slice(image_ids, (jnp.where(upper_chip, IMAGE, 0),), (1,)) >= 0
    whole = jnp.array([IMAGE, 0, 0], jnp.int32)
    parted = jnp.array([IMAGE - extra, head + lent - extra, head + lent], jnp.int32)
    limit = jnp.where(image_live, jnp.where(upper_chip, parted, whole), 0)
    valid = inside(jnp.arange(live), limit).astype(f32)[:, None]

    inputs = arranged.astype(f32)
    unit_one, inverse_one = norm_parts(inputs)
    normed_one = (unit_one * vectors[0] + vectors[1]).astype(bf16)

    def own_columns(row, part):
        return lax.dynamic_index_in_dim(row.reshape(2, 2, part), core, 1, False).reshape(-1)

    query_bias = own_columns(vectors[2], head_part)
    value_bias = own_columns(vectors[3], head_part)
    up_bias = own_columns(vectors[10:].reshape(-1), hidden_part)

    def project(matrix, bias):
        product = jnp.dot(normed_one, matrix, preferred_element_type=f32)
        return (product if bias is None else product + bias).astype(bf16)

    query = project(query_full, query_bias)
    keys = project(key_full, None)
    values = project(value_full, value_bias)
    attended, logsum = attend_forward(limit, query, keys, values, live)
    mixed = jnp.concatenate([attended, values[live:]], 0)
    attn_out = sum_cores(lax.dot_general(mixed, out_full, NT, preferred_element_type=f32))
    shifted_out = attn_out + vectors[4]
    branch_one = shifted_out * vectors[5]
    middle = inputs + branch_one
    unit_two, inverse_two = norm_parts(middle)
    normed_two = (unit_two * vectors[6] + vectors[7]).astype(bf16)

    upper = jnp.dot(normed_two, up_full, preferred_element_type=f32) + up_bias
    spread = 0.5 * (1.0 + lax.erf(upper * 0.5**0.5))
    hidden = (upper * spread).astype(bf16)
    slope = spread + upper * jnp.exp(-0.5 * upper * upper) * 0.3989422804014327
    down = sum_cores(lax.dot_general(hidden, down_full, NT, preferred_element_type=f32))
    shifted_down = down + vectors[8]
    branch_two = shifted_down * vectors[9]
    result = middle + branch_two

    seed = seeds[:live].astype(f32) * valid
    scaled_seed = seed * vectors[9]
    grad_down = scaled_seed.astype(bf16)
    live_hidden = hidden[:live]
    grad_down_weight = jnp.einsum("gd,gf->df", grad_down, live_hidden, preferred_element_type=f32)
    grad_hidden = jnp.dot(grad_down, down_full, preferred_element_type=f32)
    grad_upper = (grad_hidden * slope[:live]).astype(bf16)
    grad_up_weight = jnp.einsum(
        "gd,gf->df", normed_two[:live], grad_upper, preferred_element_type=f32
    )
    grad_normed_two = sum_cores(
        lax.dot_general(grad_upper, up_full, NT, preferred_element_type=f32)
    )
    grad_middle = seed + norm_back(
        unit_two[:live], inverse_two[:live], vectors[6], grad_normed_two
    )
    scaled_middle = grad_middle * vectors[5]
    grad_attn_out = scaled_middle.astype(bf16)
    grad_out_weight = jnp.einsum(
        "gd,gk->dk", grad_attn_out, mixed[:live], preferred_element_type=f32
    )
    grad_mixed = jnp.dot(grad_attn_out, out_full, preferred_element_type=f32).astype(bf16)
    grad_heads = attend_backward(limit, query, keys, values, grad_mixed, logsum)
    live_one = normed_one[:live]
    grad_attn = [
        jnp.einsum("gd,gk->dk", live_one, g, preferred_element_type=f32) for g in grad_heads
    ] + [grad_out_weight]
    grad_normed_one = sum_cores(
        sum(
            lax.dot_general(g, w, NT, preferred_element_type=f32)
            for g, w in zip(grad_heads, weights)
        )
    )
    grad_tokens = grad_middle + norm_back(
        unit_one[:live], inverse_one[:live], vectors[0], grad_normed_one
    )

    def own_rows(values):
        place = head + lent
        back = lax.ppermute(values[head:place], "y", ((1, 0),))
        seam = chip_rows - lent
        mine = jnp.arange(seam, chip_rows)[:, None] < IMAGE
        lower = jnp.concatenate(
            [values[local_rows:seam], jnp.where(mine, pad_rows(values)[seam:chip_rows], back)], 0
        )
        upper = jnp.concatenate([values[local_rows:head], pad_rows(values)[place:rows]], 0)
        return jnp.where(core == 0, values[:local_rows], jnp.where(upper_chip, upper, lower))

    def pad_rows(values):
        missing = jnp.zeros((rows - values.shape[0], width), values.dtype)
        return jnp.concatenate([values, missing], 0)

    block_out = own_rows(result.astype(bf16))
    grad_tokens_own = own_rows(grad_tokens)

    def square_sum(values):
        return jnp.sum(valid * values[:live] * values[:live])

    stat_terms = first_core * jnp.stack(
        [
            jnp.sum(valid),
            square_sum(middle),
            square_sum(branch_one),
            square_sum(result),
            square_sum(branch_two),
        ]
    )
    weight_local_sq = jnp.concatenate(
        [
            jnp.sum(attn_master * attn_master, axis=(1, 2)),
            jnp.sum(mlp_master * mlp_master, axis=(1, 2)),
        ]
    )

    def placed(values, part):
        zero = jnp.zeros((2, 2, part), f32)
        return lax.dynamic_update_index_in_dim(
            zero, values.reshape(2, part), core, 1
        ).reshape(-1, width)

    def column_sum(values):
        return jnp.sum(values.astype(f32), axis=0)

    shared_rows = first_core * jnp.stack(
        [
            column_sum(grad_normed_one * unit_one[:live]),
            column_sum(grad_normed_one),
            column_sum(scaled_middle),
            column_sum(grad_middle * shifted_out[:live]),
            column_sum(grad_normed_two * unit_two[:live]),
            column_sum(grad_normed_two),
            column_sum(scaled_seed),
            column_sum(seed * shifted_down[:live]),
        ]
    )
    vector_local = jnp.concatenate(
        [
            shared_rows[:2],
            placed(column_sum(grad_heads[0]), head_part),
            placed(column_sum(grad_heads[2]), head_part),
            shared_rows[2:],
            placed(column_sum(grad_upper), hidden_part),
        ],
        axis=0,
    )
    vector_total = lax.psum(vector_local, DEVICES)
    row_totals = lax.psum(stat_terms, DEVICES)
    mlp_shard = scatter_all(
        [grad_up_weight, grad_down_weight], mlp_master.shape[1], hidden_part
    )
    attn_shard = scatter_all(grad_attn, attn_master.shape[1], head_part)

    attn_first_new, attn_second_new, attn_adapted = adapt_moments(
        attn_shard, attn_first, attn_second
    )
    mlp_first_new, mlp_second_new, mlp_adapted = adapt_moments(mlp_shard, mlp_first, mlp_second)
    attn_update = attn_adapted + weight_decay * attn_master
    mlp_update = mlp_adapted + weight_decay * mlp_master
    update_local_sq = jnp.concatenate(
        [
            jnp.sum(attn_update * attn_update, axis=(1, 2)),
            jnp.sum(mlp_update * mlp_update, axis=(1, 2)),
        ]
    )
    weight_sq, update_sq = lax.psum((weight_local_sq, update_local_sq), DEVICES)
    weight_norms = jnp.sqrt(weight_sq)
    update_norms = jnp.sqrt(update_sq)
    ratios = weight_norms / update_norms
    attn_new = attn_master - learning_rate * ratios[:4, None, None] * attn_update
    mlp_new = mlp_master - learning_rate * ratios[4:, None, None] * mlp_update
    vector_first_new, vector_second_new, vector_adapted = adapt_moments(
        vector_total, vector_first, vector_second
    )
    vector_new = vectors - vector_rate * vector_adapted
    matrix_norms = jnp.stack([weight_norms, update_norms])
    row_rms = jnp.sqrt(row_totals[1:] / (row_totals[0] * width))
    return (
        block_out,
        grad_tokens_own,
        attn_shard,
        attn_new,
        attn_first_new,
        attn_second_new[:3],
        attn_second_new[3],
        attn_new.astype(bf16),
        mlp_shard,
        mlp_new,
        mlp_first_new,
        mlp_second_new,
        mlp_new.astype(bf16),
        vector_total,
        vector_new,
        vector_first_new,
        vector_second_new,
        vector_new.astype(bf16),
        matrix_norms,
        row_rms,
    )


def solution(mesh):
    outer = mesh.shape["dp"]
    chips = Mesh(mesh.devices.reshape(outer // 2, 2, 2, 2), DEVICES)
    dp = ("z", "x")
    tensor = ("y", "core")
    row_spec = P(dp + tensor, None)
    weight_spec = P(None, dp, tensor)
    in_specs = (row_spec, row_spec, P(dp)) + (weight_spec,) * 6 + (P(),) * 3
    out_specs = (
        (row_spec, row_spec)
        + (weight_spec,) * 4
        + (P(dp, tensor),)
        + (weight_spec,) * 6
        + (P(),) * 7
    )
    return jax.shard_map(
        per_device, mesh=chips, in_specs=in_specs, out_specs=out_specs, check_vma=False
    )
```

time: 1780 us -> 656 us (0.37)
  matrix products: 673 us -> 96 us
  waiting for transfers between devices: 648 us -> 125 us
  Pallas kernels: 0 us -> 231 us
  other arithmetic: 301 us -> 98.4 us
  local copies, waits for them, and re-layouts: 65.7 us -> 30.7 us
  starting transfers between devices: 0.5 us -> 29.6 us
  loops' own time: 20.5 us -> 0 us
    dot_general x54 -> x18, matrix products: 673 us -> 96 us  [the longest x1 16.9 us: per_device(): upper = jnp.dot(normed_two, up_full, preferred_element_type=f32) + up_bias]
    reduce_scatter x6 -> x0, waiting for transfers between devices: 418 us -> none  [the longest x4 356 us: sum_product(): lax.psum_scatter(jnp.einsum('sgk,sdk->gd', left_operand, right_operand, p...]
    pallas_call x0 -> x3, Pallas kernels: none -> 231 us  [the longest x1 118 us: exchange(): pl.pallas_call(functools.partial(exchange_kernel, with_weights), in_specs...]
    all_gather x6 -> x0, waiting for transfers between devices: 230 us -> none  [the longest x4 114 us: gather_rows(): return lax.all_gather(values, 'tensor', axis=0, tiled=True)]
    ppermute x0 -> x36, waiting for transfers between devices: none -> 125 us  [the longest x6 37.4 us: trade_y(): lax.ppermute(sent.astype(bf16), 'y', SWAP).astype(f32)]
    convert_element_type x15 -> x20, other arithmetic: 145 us -> 28.9 us  [the longest x1 11.7 us: per_device(): block_out = own_rows(result.astype(bf16))]
    reduce_sum x18 -> x9, other arithmetic: 98.4 us -> 34.9 us  [the longest x1 14.2 us: square_sum(): return jnp.sum(valid * values[:live] * values[:live])]
    or x12 -> x0, other arithmetic: 34 us -> none  [block_scores(): allowed = same_image | (row_position[:, None] == column_position[None, :])]
  transfers between devices with their start and end apart: 12 -> 36, of which waited for: 10 -> 24; matrix products, arithmetic and copies ran while one was open for 41% -> 17% of each run, Pallas kernels for 0% -> 10%
where the time goes in v1:
time: 656 us; the launch traced here: 652 us
  Pallas kernels  231 us (35%)
  waiting for transfers between devices  125 us (19%)
  other arithmetic  98.4 us (15%)
  matrix products  96 us (15%)
  blocking collectives  38.2 us (6%)
  local copies, waits for them, and re-layouts  30.7 us (5%)
  starting transfers between devices  29.6 us (5%)
    pallas_call x1, Pallas kernels, exchange(): pl.pallas_call(functools.partial(exchange_kernel, with_weights), in_specs...  118 us
    pallas_call x1, Pallas kernels, attend_backward(): pl.pallas_call(attend_backward_kernel, grid_spec=pltpu.PrefetchScalarGrid...  68.2 us
    pallas_call x1, Pallas kernels, attend_forward(): pl.pallas_call(attend_forward_kernel, grid_spec=pltpu.PrefetchScalarGridS...  45.3 us
    psum x1, blocking collectives, per_device(): weight_sq, update_sq = lax.psum((weight_local_sq, update_local_sq), DEVICES)  38.2 us
    ppermute x6, waiting for transfers between devices, trade_y(): lax.ppermute(sent.astype(bf16), 'y', SWAP).astype(f32)  37.4 us
    ppermute x18, waiting for transfers between devices, scatter_short(): moving = lax.ppermute(moving.astype(bf16), 'z', ring).astype(f32)  31.1 us
    ppermute x6, waiting for transfers between devices, trade_x(): lax.ppermute(sent.astype(bf16), 'x', SWAP).astype(f32)  28.1 us
    ppermute x2, waiting for transfers between devices, own_rows(): back = lax.ppermute(values[head:place], 'y', ((1, 0),))  28 us
  transfers between devices with their start and end apart: 36, of which 24 were waited for; matrix products, arithmetic and copies ran while one was open for 17% of the time, Pallas kernels for 10%

profile of v1, /device:TPU:0, one launch (start us, length us, event | category | flops | bytes accessed | tf_op | source)
XLA Modules:
  0.0 652.0 jit_solution(9875792076522235465)
XLA Ops:
  0.7 2.1 convert_element_type.327.mlp_ref
  2.8 1.8 convert_element_type.326.attn_ref
  4.5 117.9 %exchange.1 = (bf16[1712,1024]{1,0:T(8,128)(2,1)}, bf16[1712,1024]{1,0:T(8,128)(2,1)}, bf16[4,2,128,512]{3,2,1,0:T(8,128)(2,1)}, bf16[4,2,128,512]{3,2,1,0:T(8,1...) custom-call(bf16[768,1024]{1,0:T(8,128)(2,1)} %tokens_ref.1, ...), custom_call_target="tpu_custom_call" | custom-call | tf_op jit(solution)/shard_map/exchange/pallas_call | solution.py:458
  122.5 2.7 convert_reduce_fusion.1
  127.3 3.8 fusion.6
  131.1 2.0 convolution_convert_fusion.4.k_ref
  133.2 2.1 add_convert_fusion.3.v_ref.own_ref
  136.5 2.1 add_convert_fusion.4.q_ref
  140.6 45.3 %attend_forward.1 = (bf16[1408,512]{1,0:T(8,128)(2,1)S(1)}, f32[1408,512]{1,0:T(8,128)}) custom-call(s32[3]{0:T(128)S(1)} %broadcast_select_fusion.1.limit_ref, bf16[1712,512]{1,0:T(8,128)(2,1)S(1)} %add_convert_fusion.4.q_ref, bf16[1712,512]{1,0:T(8,128)(2,1)S(1)} %convolution_convert_fusion.4.k_ref, bf16[1712,512]{1,0:T(8,128)(2,1)} %copy-done.36, ...), custom_call_target="tpu_custom_call" | custom-call | flops 8120172544 | bytes 5767168 | tf_op jit(solution)/shard_map/attend_forward/pallas_call | solution.py:85
  186.0 3.8 convolution_convert_fusion.2
  189.8 9.1 %collective-permute-start = (bf16[1712,1024]{1,0:T(8,128)(2,1)}, bf16[1712,1024]{1,0:T(8,128)(2,1)}, u32[]{:S(2)}, u32[]{:S(2)}) collective-permute-start(bf16[1712,1024]{1,0:T(8,128)(2,1)} %convolution_convert_fusion.2), channel_id=1, source_target_pairs={{0,1},{1,0},{2,3},{3,2},{4,5},{5,4},{6,7},{7,6},{8,9},{9,8},{10,11... | collective-permute-start | bytes 10518536 | tf_op jit(solution)/shard_map/ppermute | solution.py:208
  200.3 2.5 fusion.77
  203.3 1.9 fusion.75
  205.3 8.0 %fusion.86 = (f32[1712]{0:T(1024)S(1)}, f32[1712,1024]{1,0:T(8,128)S(1)}, f32[1712,1024]{1,0:T(8,128)}, f32[1712,1024]{1,0:T(8,128)}) fusion(bf16[1712,1024]{1,0:T(8,128)(2,1)S(1)} %copy-done.6, f32[1024]{0:T(1024)S(1)} %bitcast.241, f32[1024]{0:T(1024)} %bitcast.257, bf16[1712,1024]{1,0:T(8,128)(2,1)} %collective-permute-done, ...), kind=kLoop, calls=%fused_computation.233 | loop fusion | flops 14022992 | bytes 31570624 | tf_op jit(solution)/shard_map/reduce_sum | solution.py:185
  214.2 4.0 add_convert_fusion
  218.3 16.9 %multiply_convert_fusion = (bf16[1712,2048]{1,0:T(8,128)(2,1)}, f32[1712,2048]{1,0:T(8,128)}, f32[1712,2048]{1,0:T(8,128)}) fusion(f32[2048]{0:T(1024)S(1)} %bitcast.264, bf16[1712,1024]{1,0:T(8,128)(2,1)S(1)} %get-tuple-element.95, bf16[1024,2048]{1,0:T(8,128)(2,1)} %bitcast.269), kind=kOutput, calls=%fused_computation.1 | convolution fusion | flops 7201685504 | bytes 42770432 | tf_op jit(solution)/shard_map/dot_general | solution.py:575
  235.2 15.7 %convert_reduce_fusion = (f32[2048]{0:T(1024)S(1)}, bf16[1408,2048]{1,0:T(8,128)(2,1)}) fusion(f32[1712,2048]{1,0:T(8,128)} %get-tuple-element.122, f32[1712,2048]{1,0:T(8,128)} %get-tuple-element.94, bf16[1024,2048]{1,0:T(8,128)(2,1)} %bitcast.267, f32[1024]{0:T(1024)S(1)} %bitcast.245, f32[1408]{0:T(1024)S(1)} %fusion.75, bf16[1712,1024]{1,0:T(8,128)(2,1)S(1)} %copy-done.24), kind=kOutput, calls=%fused_computation.9 | convolution fusion | flops 5937297408 | bytes 35934208 | tf_op jit(solution)/shard_map/dot_general | solution.py:589
  250.9 10.5 %convolution_convert_fusion = bf16[1408,1024]{1,0:T(8,128)(2,1)S(1)} fusion(bf16[1408,2048]{1,0:T(8,128)(2,1)} %get-tuple-element.124, bf16[1024,2048]{1,0:T(8,128)(2,1)} %bitcast.270), kind=kOutput, calls=%fused_computation.64 | convolution fusion | flops 5907021824 | bytes 12845056 | tf_op jit(solution)/shard_map/dot_general | solution.py:595
  261.4 6.8 %fusion.26 = f32[1024,2048]{1,0:T(8,128)S(1)} fusion(bf16[1408,2048]{1,0:T(8,128)(2,1)S(1)} %copy-done.59, bf16[1712,1024]{1,0:T(8,128)(2,1)S(1)} %get-tuple-element.95), kind=kOutput, calls=%fused_computation.75 | convolution fusion | flops 5905580032 | bytes 17039360 | tf_op jit(solution)/shard_map/gd,gf->df/dot_general | solution.py:591
  268.3 3.2 copy-done.15
  271.5 1.7 fusion.34
  274.6 7.3 %fusion.15 = f32[1024,2048]{1,0:T(8,128)S(1)} fusion(bf16[1712,2048]{1,0:T(8,128)(2,1)S(1)} %copy-done.60, f32[1024]{0:T(1024)S(1)} %bitcast.246, f32[1408]{0:T(1024)S(1)} %fusion.75, bf16[1712,1024]{1,0:T(8,128)(2,1)S(1)} %copy-done.24), kind=kOutput, calls=%fused_computation.37 | convolution fusion | flops 5911347200 | bytes 17051648 | tf_op jit(solution)/shard_map/gd,gf->df/dot_general | solution.py:588
  282.3 1.6 copy.58
  283.9 3.0 copy-done.16
  287.4 9.2 %convolution_convert_fusion.1 = bf16[1712,1024]{1,0:T(8,128)(2,1)} fusion(bf16[1712,2048]{1,0:T(8,128)(2,1)S(1)} %copy-done.60, bf16[1024,2048]{1,0:T(8,128)(2,1)S(1)} %bitcast.268), kind=kOutput, calls=%fused_computation.65 | convolution fusion | flops 7182401536 | bytes 14712832 | tf_op jit(solution)/shard_map/dot_general | solution.py:579
  296.7 24.3 %collective-permute-done.26 = bf16[4,128,2048]{2,1,0:T(8,128)(2,1)} collective-permute-done((bf16[4,128,2048]{2,1,0:T(8,128)(2,1)}, bf16[4,128,2048]{2,1,0:T(8,128)(2,1)}, u32[]{:S(2)}, u32[]{:S(2)}) %collective-permute-start.26) | collective-permute-done | bytes 2097184 | tf_op jit(solution)/shard_map/ppermute | solution.py:494
  321.0 3.4 bitcast_add_fusion
  325.2 10.5 %collective-permute-done.31 = bf16[4,2,128,1024]{3,2,0,1:T(8,128)(2,1)} collective-permute-done((bf16[4,2,128,1024]{3,2,0,1:T(8,128)(2,1)}, bf16[4,2,128,1024]{3,2,0,1:T(8,128)(2,1)}, u32[]{:S(2)}, u32[]{:S(2)}) %collective-permute-start.31) | collective-permute-done | bytes 2097184 | tf_op jit(solution)/shard_map/ppermute | solution.py:489
  335.7 2.6 copy_add_fusion
  339.1 3.9 multiply_reduce_fusion.1
  343.0 13.8 %collective-permute-done.27 = bf16[4,128,1024]{2,1,0:T(8,128)(2,1)S(1)} collective-permute-done((bf16[4,128,1024]{2,1,0:T(8,128)(2,1)S(1)}, bf16[4,128,1024]{2,1,0:T(8,128)(2,1)S(1)}, u32[]{:S(2)}, u32[]{:S(2)}) %collective-permute-start.27) | collective-permute-done | bytes 1048608 | tf_op jit(solution)/shard_map/ppermute | solution.py:489
  357.4 3.8 collective-permute-done.32
  361.9 6.5 %collective-permute-done.28 = bf16[128,1024]{1,0:T(8,128)(2,1)S(1)} collective-permute-done((bf16[128,1024]{1,0:T(8,128)(2,1)S(1)}, bf16[128,1024]{1,0:T(8,128)(2,1)S(1)}, u32[]{:S(2)}, u32[]{:S(2)}) %collective-permute-start.28) | collective-permute-done | bytes 262176 | tf_op jit(solution)/shard_map/ppermute | solution.py:501
  369.2 4.9 collective-permute-done.33
  374.8 11.7 %fusion.85 = (bf16[1712,1024]{1,0:T(8,128)(2,1)}, f32[1712,1024]{1,0:T(8,128)}, f32[1712,1024]{1,0:T(8,128)}, f32[1712,1024]{1,0:T(8,128)}) fusion(f32[1712,1024]{1,0:T(8,128)S(1)} %bitcast.212, f32[1024]{0:T(1024)S(1)} %bitcast.247, f32[1024]{0:T(1024)S(1)} %bitcast.255, bf16[1712,1024]{1,0:T(8,128)(2,1)} %collective-permute-done.1, ...), kind=kLoop, calls=%fused_computation.232 | loop fusion | flops 12271616 | bytes 38576128 | tf_op jit(solution)/shard_map/convert_element_type | solution.py:636
  386.6 14.2 %fusion.12 = (f32[]{:T(128)}, f32[]{:T(128)}, f32[]{:T(128)}, f32[]{:T(128)}, f32[1024]{0:T(1024)S(1)}, /*index=5*/f32[1024]{0:T(1024)S(1)}, f32[1024]{0:T(1024)S(1)}, f32[1024]{0:T(1024)S(1)}, f32[1408,1024]{1,0:T(8,128)S(1)}) fusion(f32[1712,1024]{1,0:T(8,128)} %get-tuple-element.91, f32[1408]{0:T(1024)S(1)} %fusion.75, f32[1712,1024]{1,0:T(8,128)S(1)} %bitcast.212, ...), kind=kLoop, calls=%fused_computation.32 | loop fusion | flops 44691452 | bytes 54839312 | tf_op jit(solution)/shard_map/reduce_sum | solution.py:640
  400.8 1.7 convolution_convert_fusion.3.grad_ref
  403.3 68.2 %attend_backward.1 = (bf16[1408,512]{1,0:T(8,128)(2,1)S(1)}, bf16[1408,512]{1,0:T(8,128)(2,1)S(1)}, bf16[1408,512]{1,0:T(8,128)(2,1)S(1)}) custom-call(s32[3]{0:T(128)S(1)} %broadcast_select_fusion.1.limit_ref, bf16[1712,512]{1,0:T(8,128)(2,1)} %copy-done.3, bf16[1712,512]{1,0:T(8,128)(2,1)} %copy-done.2, bf16[1712,512]{1,0:T(8,128)(2,1)} %copy-done.36, ...), custom_call_target="tpu_custom_call" | custom-call | flops 20300431360 | bytes 11534336 | tf_op jit(solution)/shard_map/attend_backward/pallas_call | solution.py:156
  471.5 1.7 fusion.89
  473.5 3.1 fusion.32
  476.6 1.7 fusion.90
  478.3 3.2 fusion.30
  481.8 3.1 fusion.28
  485.0 3.1 fusion.38
  488.1 1.9 add_convert_fusion.2
  493.3 3.3 stack.103
  506.0 14.6 %collective-permute-done.2 = bf16[176,1024]{1,0:T(8,128)(2,1)S(1)} collective-permute-done((bf16[176,1024]{1,0:T(8,128)(2,1)S(1)}, bf16[176,1024]{1,0:T(8,128)(2,1)S(1)}, u32[]{:S(2)}, u32[]{:S(2)}) %collective-permute-start.2) | collective-permute-done | bytes 360480 | tf_op jit(solution)/shard_map/ppermute | solution.py:623
  520.9 2.3 slice_select_fusion.1
  524.8 5.6 collective-permute-done.35
  530.5 2.5 multiply_reduce_fusion.7
  534.4 2.1 collective-permute-start.7
  536.7 1.6 collective-permute-start.12
  538.6 6.6 %collective-permute-done.21 = bf16[4,2,128,256]{3,2,0,1:T(8,128)(2,1)S(1)} collective-permute-done((bf16[4,2,128,256]{3,2,0,1:T(8,128)(2,1)S(1)}, bf16[4,2,128,256]{3,2,0,1:T(8,128)(2,1)S(1)}, u32[]{:S(2)}, u32[]{:S(2)}) %collective-permute-start.21) | collective-permute-done | bytes 524320 | tf_op jit(solution)/shard_map/ppermute | solution.py:489
  546.9 3.8 collective-permute-done.7
  551.5 2.7 collective-permute-done.17
  554.5 1.9 collective-permute-start.23
  562.7 1.6 collective-permute-done.9
  571.8 1.9 collective-permute-done.20
  577.7 3.8 multiply_reduce_fusion.2
  583.8 38.2 %all-reduce.1 = (f32[6]{0:T(128)S(1)}, f32[6]{0:T(128)S(1)}, f32[14,1024]{1,0:T(8,128)}, f32[5]{0:T(128)S(1)}) all-reduce(f32[6]{0:T(128)} %pad_maximum_fusion.4, f32[6]{0:T(128)} %pad_maximum_fusion.3, f32[14,1024]{1,0:T(8,128)S(1)} %concatenate.36, ...), channel_id=1, replica_groups=mesh['z'=4,'x'=2,'y'=2,'core'=2] {'z','x','y','core'}, use_global_device_ids=true, to_apply=%region_13.14 | all-reduce | flops 14353 | bytes 114824 | tf_op jit(solution)/shard_map/psum | solution.py:708
  622.1 6.3 multiply_add_fusion
  633.8 1.8 fusion.81
  635.6 13.4 %collective-permute-done.5 = f32[176,1024]{1,0:T(8,128)S(1)} collective-permute-done((f32[176,1024]{1,0:T(8,128)S(1)}, f32[176,1024]{1,0:T(8,128)S(1)}, u32[]{:S(2)}, u32[]{:S(2)}) %collective-permute-start.5) | collective-permute-done | bytes 720928 | tf_op jit(solution)/shard_map/ppermute | solution.py:623
  649.1 2.7 slice_select_fusion
  (303 shorter events, 60.1 us)
Async XLA Ops:
  138.6 47.3 %copy-start.3 = (bf16[1712,512]{1,0:T(8,128)(2,1)}, bf16[1712,512]{1,0:T(8,128)(2,1)S(1)}, u32[]{:S(2)}) copy-start(bf16[1712,512]{1,0:T(8,128)(2,1)S(1)} %add_convert_fusion.4.q_ref) | copy-start | bytes 5259268
  140.6 45.3 %slice-start.8 = ((bf16[1712,512]{1,0:T(8,128)(2,1)}), bf16[304,512]{1,0:T(8,128)(2,1)S(1)}, s32[]{:S(2)}) async-start(bf16[1712,512]{1,0:T(8,128)(2,1)} %copy-done.36), calls=%async_computation.8 | async-start | bytes 622592 | tf_op jit(solution)/shard_map/slice | solution.py:567
  140.6 45.3 %copy-start.57 = (bf16[4,2,128,512]{3,2,1,0:T(8,128)(2,1)S(1)}, bf16[4,2,128,512]{3,2,1,0:T(8,128)(2,1)}, u32[]{:S(2)}) copy-start(bf16[4,2,128,512]{3,2,1,0:T(8,128)(2,1)} %get-tuple-element.38) | copy-start | bytes 3145732
  185.9 19.4 %copy-start.6 = (bf16[1712,1024]{1,0:T(8,128)(2,1)S(1)}, bf16[1712,1024]{1,0:T(8,128)(2,1)}, u32[]{:S(2)}) copy-start(bf16[1712,1024]{1,0:T(8,128)(2,1)} %get-tuple-element.33) | copy-start | bytes 10518532
  189.8 15.6 %collective-permute-start = (bf16[1712,1024]{1,0:T(8,128)(2,1)}, bf16[1712,1024]{1,0:T(8,128)(2,1)}, u32[]{:S(2)}, u32[]{:S(2)}) collective-permute-start(bf16[1712,1024]{1,0:T(8,128)(2,1)} %convolution_convert_fusion.2), channel_id=1, source_target_pairs={{0,1},{1,0},{2,3},{3,2},{4,5},{5,4},{6,7},{7,6},{8,9},{9,8},{10,11... | collective-permute-start | bytes 10518536 | tf_op jit(solution)/shard_map/ppermute | solution.py:208
  218.2 16.9 %copy-start.24 = (bf16[1712,1024]{1,0:T(8,128)(2,1)S(1)}, bf16[1712,1024]{1,0:T(8,128)(2,1)}, u32[]{:S(2)}) copy-start(bf16[1712,1024]{1,0:T(8,128)(2,1)} %get-tuple-element.41) | copy-start | bytes 10518532
  250.8 10.5 %copy-start.59 = (bf16[1408,2048]{1,0:T(8,128)(2,1)S(1)}, bf16[1408,2048]{1,0:T(8,128)(2,1)}, u32[]{:S(2)}) copy-start(bf16[1408,2048]{1,0:T(8,128)(2,1)} %get-tuple-element.124) | copy-start | bytes 17301508
  261.4 13.3 %copy-start.60 = (bf16[1712,2048]{1,0:T(8,128)(2,1)S(1)}, bf16[1712,2048]{1,0:T(8,128)(2,1)}, u32[]{:S(2)}) copy-start(bf16[1712,2048]{1,0:T(8,128)(2,1)} %get-tuple-element.93) | copy-start | bytes 21037060
  268.2 70.9 %collective-permute-start.3 = (bf16[1408,1024]{1,0:T(8,128)(2,1)S(1)}, bf16[1408,1024]{1,0:T(8,128)(2,1)}, u32[]{:S(2)}, u32[]{:S(2)}) collective-permute-start(bf16[1408,1024]{1,0:T(8,128)(2,1)S(1)} %convolution_convert_fusion), channel_id=1, source_target_pairs={{0,1},{1,0},{2,3},{3,2},{4,5},{5,4},{6,7},{7,6},{8,9},{9,8},{10,11... | collective-permute-start | bytes 8650760 | tf_op jit(solution)/shard_map/ppermute | solution.py:208
  273.1 47.9 %collective-permute-start.26 = (bf16[4,128,2048]{2,1,0:T(8,128)(2,1)}, bf16[4,128,2048]{2,1,0:T(8,128)(2,1)}, u32[]{:S(2)}, u32[]{:S(2)}) collective-permute-start(bf16[4,128,2048]{2,1,0:T(8,128)(2,1)} %fusion.34), channel_id=1, source_target_pairs={{0,4},{4,0},{1,5},{5,1},{2,6},{6,2},{3,7},{7,3},{8,12},{12,8},{9,1... | collective-permute-start | bytes 6291464 | tf_op jit(solution)/shard_map/ppermute | solution.py:494
  286.9 48.8 %collective-permute-start.31 = (bf16[4,2,128,1024]{3,2,0,1:T(8,128)(2,1)}, bf16[4,2,128,1024]{3,2,0,1:T(8,128)(2,1)}, u32[]{:S(2)}, u32[]{:S(2)}) collective-permute-start(bf16[4,2,128,1024]{3,2,0,1:T(8,128)(2,1)} %copy.58), channel_id=1, source_target_pairs={{0,2},{2,0},{1,3},{3,1},{4,6},{6,4},{5,7},{7,5},{8,10},{10,8},{9,1... | collective-permute-start | bytes 6291464 | tf_op jit(solution)/shard_map/ppermute | solution.py:489
  296.6 78.2 %collective-permute-start.1 = (bf16[1712,1024]{1,0:T(8,128)(2,1)}, bf16[1712,1024]{1,0:T(8,128)(2,1)}, u32[]{:S(2)}, u32[]{:S(2)}) collective-permute-start(bf16[1712,1024]{1,0:T(8,128)(2,1)} %convolution_convert_fusion.1), channel_id=1, source_target_pairs={{0,1},{1,0},{2,3},{3,2},{4,5},{5,4},{6,7},{7,6},{8,9},{9,8},{10,11... | collective-permute-start | bytes 10518536 | tf_op jit(solution)/shard_map/ppermute | solution.py:208
  296.7 39.0 %copy-start.17 = (f32[1024,2048]{1,0:T(8,128)S(1)}, f32[1024,2048]{1,0:T(8,128)}, u32[]{:S(2)}) copy-start(f32[1024,2048]{1,0:T(8,128)} %copy-done.16) | copy-start | bytes 25165828
  324.4 14.6 %slice-start.2 = ((s8[7012352]{0:T(1024)(128)(4,1)}), s8[4194304]{0:T(1024)(128)(4,1)S(1)}, s32[]{:S(2)}) async-start(s8[7012352]{0:T(1024)(128)(4,1)} %bitcast.213), calls=%async_computation.2 | async-start | bytes 8388608
  324.6 14.5 %slice-start.3 = ((s8[7012352]{0:T(1024)(128)(4,1)}), s8[2818048]{0:T(1024)(128)(4,1)S(1)}, s32[]{:S(2)}) async-start(s8[7012352]{0:T(1024)(128)(4,1)} %bitcast.213), calls=%async_computation.3 | async-start | bytes 5636096
  324.6 32.2 %collective-permute-start.27 = (bf16[4,128,1024]{2,1,0:T(8,128)(2,1)S(1)}, bf16[4,128,1024]{2,1,0:T(8,128)(2,1)S(1)}, u32[]{:S(2)}, u32[]{:S(2)}) collective-permute-start(bf16[4,128,1024]{2,1,0:T(8,128)(2,1)S(1)} %dynamic-slice_convert_fusion.1), channel_id=1, source_target_pairs={{0,2},{2,0},{1,3},{3,1},{4,6},{6,4},{5,7},{7,5},{8,10},{10,8},{9,1... | collective-permute-start | bytes 3145736 | tf_op jit(solution)/shard_map/ppermute | solution.py:489
  338.5 22.8 %collective-permute-start.32 = (bf16[4,128,1024]{2,1,0:T(8,128)(2,1)S(1)}, bf16[4,128,1024]{2,1,0:T(8,128)(2,1)S(1)}, u32[]{:S(2)}, u32[]{:S(2)}) collective-permute-start(bf16[4,128,1024]{2,1,0:T(8,128)(2,1)S(1)} %fusion.40), channel_id=1, source_target_pairs={{0,4},{4,0},{1,5},{5,1},{2,6},{6,2},{3,7},{7,3},{8,12},{12,8},{9,1... | collective-permute-start | bytes 3145736 | tf_op jit(solution)/shard_map/ppermute | solution.py:494
  356.8 18.0 %slice-start = ((s8[7012352]{0:T(1024)(128)(4,1)}), s8[4194304]{0:T(1024)(128)(4,1)S(1)}, s32[]{:S(2)}) async-start(s8[7012352]{0:T(1024)(128)(4,1)} %bitcast.211), calls=%async_computation | async-start | bytes 8388608
  357.3 17.5 %copy-start.11 = (f32[4,128,1024]{2,1,0:T(8,128)}, f32[4,128,1024]{2,1,0:T(8,128)S(1)}, u32[]{:S(2)}) copy-start(f32[4,128,1024]{2,1,0:T(8,128)S(1)} %convert_add_fusion.3) | copy-start | bytes 6291460
  357.3 17.5 %copy-start.46 = (f32[1,1024]{1,0:T(1,128)S(1)}, f32[1,1024]{1,0:T(1,128)}, u32[]{:S(2)}) copy-start(f32[1,1024]{1,0:T(1,128)} %get-tuple-element.110) | copy-start | bytes 12292
  357.4 17.5 %slice-start.1 = ((s8[7012352]{0:T(1024)(128)(4,1)}), s8[2818048]{0:T(1024)(128)(4,1)S(1)}, s32[]{:S(2)}) async-start(s8[7012352]{0:T(1024)(128)(4,1)} %bitcast.211), calls=%async_computation.1 | async-start | bytes 5636096
  357.4 11.0 %collective-permute-start.28 = (bf16[128,1024]{1,0:T(8,128)(2,1)S(1)}, bf16[128,1024]{1,0:T(8,128)(2,1)S(1)}, u32[]{:S(2)}, u32[]{:S(2)}) collective-permute-start(bf16[128,1024]{1,0:T(8,128)(2,1)S(1)} %fusion.55), channel_id=1, source_target_pairs={{0,8},{8,16},{16,24},{24,0},{1,9},{9,17},{17,25},{25,1},{2,10},{10... | collective-permute-start | bytes 786440 | tf_op jit(solution)/shard_map/ppermute | solution.py:501
  361.7 13.1 %copy-start.13 = (f32[4,128,1024]{2,1,0:T(8,128)}, f32[4,128,1024]{2,1,0:T(8,128)S(1)}, u32[]{:S(2)}) copy-start(f32[4,128,1024]{2,1,0:T(8,128)S(1)} %bitcast_add_fusion.1) | copy-start | bytes 6291460
  361.8 12.2 %collective-permute-start.33 = (bf16[128,1024]{1,0:T(8,128)(2,1)S(1)}, bf16[128,1024]{1,0:T(8,128)(2,1)S(1)}, u32[]{:S(2)}, u32[]{:S(2)}) collective-permute-start(bf16[128,1024]{1,0:T(8,128)(2,1)S(1)} %fusion.56), channel_id=1, source_target_pairs={{0,8},{8,16},{16,24},{24,0},{1,9},{9,17},{17,25},{25,1},{2,10},{10... | collective-permute-start | bytes 786440 | tf_op jit(solution)/shard_map/ppermute | solution.py:501
  369.2 133.2 %collective-permute-start.29 = (bf16[128,1024]{1,0:T(8,128)(2,1)}, bf16[128,1024]{1,0:T(8,128)(2,1)}, u32[]{:S(2)}, u32[]{:S(2)}) collective-permute-start(bf16[128,1024]{1,0:T(8,128)(2,1)} %fusion.50), channel_id=1, source_target_pairs={{0,8},{8,16},{16,24},{24,0},{1,9},{9,17},{17,25},{25,1},{2,10},{10... | collective-permute-start | bytes 786440 | tf_op jit(solution)/shard_map/ppermute | solution.py:501
  374.8 130.1 %collective-permute-start.34 = (bf16[128,1024]{1,0:T(8,128)(2,1)}, bf16[128,1024]{1,0:T(8,128)(2,1)}, u32[]{:S(2)}, u32[]{:S(2)}) collective-permute-start(bf16[128,1024]{1,0:T(8,128)(2,1)} %fusion.47), channel_id=1, source_target_pairs={{0,8},{8,16},{16,24},{24,0},{1,9},{9,17},{17,25},{25,1},{2,10},{10... | collective-permute-start | bytes 786440 | tf_op jit(solution)/shard_map/ppermute | solution.py:501
  386.6 14.2 %copy-start.58 = (bf16[4,2,128,512]{3,2,1,0:T(8,128)(2,1)S(1)}, bf16[4,2,128,512]{3,2,1,0:T(8,128)(2,1)}, u32[]{:S(2)}) copy-start(bf16[4,2,128,512]{3,2,1,0:T(8,128)(2,1)} %get-tuple-element.38) | copy-start | bytes 3145732
  403.3 68.2 %copy-start.56 = (bf16[4,2,128,512]{3,2,1,0:T(8,128)(2,1)S(1)}, bf16[4,2,128,512]{3,2,1,0:T(8,128)(2,1)}, u32[]{:S(2)}) copy-start(bf16[4,2,128,512]{3,2,1,0:T(8,128)(2,1)} %get-tuple-element.34) | copy-start | bytes 3145732
  490.1 87.6 %collective-permute-start.4 = (bf16[1408,1024]{1,0:T(8,128)(2,1)S(1)}, bf16[1408,1024]{1,0:T(8,128)(2,1)}, u32[]{:S(2)}, u32[]{:S(2)}) collective-permute-start(bf16[1408,1024]{1,0:T(8,128)(2,1)S(1)} %add_convert_fusion.2), channel_id=1, source_target_pairs={{0,1},{1,0},{2,3},{3,2},{4,5},{5,4},{6,7},{7,6},{8,9},{9,8},{10,11... | collective-permute-start | bytes 8650760 | tf_op jit(solution)/shard_map/ppermute | solution.py:208
  492.7 40.2 %collective-permute-start.6 = (bf16[4,128,512]{2,1,0:T(8,128)(2,1)S(1)}, bf16[4,128,512]{2,1,0:T(8,128)(2,1)}, u32[]{:S(2)}, u32[]{:S(2)}) collective-permute-start(bf16[4,128,512]{2,1,0:T(8,128)(2,1)S(1)} %fusion.43), channel_id=1, source_target_pairs={{0,4},{4,0},{1,5},{5,1},{2,6},{6,2},{3,7},{7,3},{8,12},{12,8},{9,1... | collective-permute-start | bytes 1572872 | tf_op jit(solution)/shard_map/ppermute | solution.py:494
  498.8 37.7 %collective-permute-start.11 = (bf16[4,2,128,256]{3,2,0,1:T(8,128)(2,1)S(1)}, bf16[4,2,128,256]{3,2,0,1:T(8,128)(2,1)S(1)}, u32[]{:S(2)}, u32[]{:S(2)}) collective-permute-start(bf16[4,2,128,256]{3,2,0,1:T(8,128)(2,1)S(1)} %copy.60), channel_id=1, source_target_pairs={{0,2},{2,0},{1,3},{3,1},{4,6},{6,4},{5,7},{7,5},{8,10},{10,8},{9,1... | collective-permute-start | bytes 1572872 | tf_op jit(solution)/shard_map/ppermute | solution.py:489
  502.1 18.6 %copy-start.48 = (pred[176]{0:T(512)(128)(4,1)S(1)}, pred[176]{0:T(512)(128)(4,1)}, u32[]{:S(2)}) copy-start(pred[176]{0:T(512)(128)(4,1)} %add_compare_fusion) | copy-start | bytes 532
  502.4 18.2 %collective-permute-start.2 = (bf16[176,1024]{1,0:T(8,128)(2,1)S(1)}, bf16[176,1024]{1,0:T(8,128)(2,1)S(1)}, u32[]{:S(2)}, u32[]{:S(2)}) collective-permute-start(bf16[176,1024]{1,0:T(8,128)(2,1)S(1)} %slice.218), channel_id=1, source_target_pairs={{2,0},{3,1},{6,4},{7,5},{10,8},{11,9},{14,12},{15,13},{18,16},{19,... | collective-permute-start | bytes 1081352 | tf_op jit(solution)/shard_map/ppermute | solution.py:623
  504.9 18.3 %collective-permute-start.30 = (bf16[128,1024]{1,0:T(8,128)(2,1)S(1)}, bf16[128,1024]{1,0:T(8,128)(2,1)S(1)}, u32[]{:S(2)}, u32[]{:S(2)}) collective-permute-start(bf16[128,1024]{1,0:T(8,128)(2,1)S(1)} %fusion.49), channel_id=1, source_target_pairs={{0,8},{8,16},{16,24},{24,0},{1,9},{9,17},{17,25},{25,1},{2,10},{10... | collective-permute-start | bytes 786440 | tf_op jit(solution)/shard_map/ppermute | solution.py:501
  520.6 9.8 %collective-permute-start.35 = (bf16[128,1024]{1,0:T(8,128)(2,1)S(1)}, bf16[128,1024]{1,0:T(8,128)(2,1)S(1)}, u32[]{:S(2)}, u32[]{:S(2)}) collective-permute-start(bf16[128,1024]{1,0:T(8,128)(2,1)S(1)} %fusion.46), channel_id=1, source_target_pairs={{0,8},{8,16},{16,24},{24,0},{1,9},{9,17},{17,25},{25,1},{2,10},{10... | collective-permute-start | bytes 786440 | tf_op jit(solution)/shard_map/ppermute | solution.py:501
  520.9 9.6 %copy-start.9 = (f32[2,128,1024]{2,1,0:T(8,128)S(1)}, f32[2,128,1024]{2,1,0:T(8,128)}, u32[]{:S(2)}) copy-start(f32[2,128,1024]{2,1,0:T(8,128)} %param.20) | copy-start | bytes 3145732
  523.2 15.0 %collective-permute-start.16 = (bf16[4,128,512]{2,1,0:T(8,128)(2,1)S(1)}, bf16[4,128,512]{2,1,0:T(8,128)(2,1)S(1)}, u32[]{:S(2)}, u32[]{:S(2)}) collective-permute-start(bf16[4,128,512]{2,1,0:T(8,128)(2,1)S(1)} %fusion.44), channel_id=1, source_target_pairs={{0,4},{4,0},{1,5},{5,1},{2,6},{6,2},{3,7},{7,3},{8,12},{12,8},{9,1... | collective-permute-start | bytes 1572872 | tf_op jit(solution)/shard_map/ppermute | solution.py:494
  530.4 14.8 %collective-permute-start.21 = (bf16[4,2,128,256]{3,2,0,1:T(8,128)(2,1)S(1)}, bf16[4,2,128,256]{3,2,0,1:T(8,128)(2,1)S(1)}, u32[]{:S(2)}, u32[]{:S(2)}) collective-permute-start(bf16[4,2,128,256]{3,2,0,1:T(8,128)(2,1)S(1)} %copy.59), channel_id=1, source_target_pairs={{0,2},{2,0},{1,3},{3,1},{4,6},{6,4},{5,7},{7,5},{8,10},{10,8},{9,1... | collective-permute-start | bytes 1572872 | tf_op jit(solution)/shard_map/ppermute | solution.py:489
  532.9 12.2 %copy-start.26 = (f32[1024,512]{1,0:T(8,128)S(1)}, f32[1024,512]{1,0:T(8,128)}, u32[]{:S(2)}) copy-start(f32[1024,512]{1,0:T(8,128)} %fusion.38) | copy-start | bytes 6291460
  534.4 16.4 %collective-permute-start.7 = (bf16[4,128,256]{2,1,0:T(8,128)(2,1)S(1)}, bf16[4,128,256]{2,1,0:T(8,128)(2,1)S(1)}, u32[]{:S(2)}, u32[]{:S(2)}) collective-permute-start(bf16[4,128,256]{2,1,0:T(8,128)(2,1)S(1)} %dynamic-slice_convert_fusion.7), channel_id=1, source_target_pairs={{0,2},{2,0},{1,3},{3,1},{4,6},{6,4},{5,7},{7,5},{8,10},{10,8},{9,1... | collective-permute-start | bytes 786440 | tf_op jit(solution)/shard_map/ppermute | solution.py:489
  536.7 14.3 %collective-permute-start.12 = (bf16[4,128,256]{2,1,0:T(8,128)(2,1)S(1)}, bf16[4,128,256]{2,1,0:T(8,128)(2,1)S(1)}, u32[]{:S(2)}, u32[]{:S(2)}) collective-permute-start(bf16[4,128,256]{2,1,0:T(8,128)(2,1)S(1)} %fusion.53), channel_id=1, source_target_pairs={{0,4},{4,0},{1,5},{5,1},{2,6},{6,2},{3,7},{7,3},{8,12},{12,8},{9,1... | collective-permute-start | bytes 786440 | tf_op jit(solution)/shard_map/ppermute | solution.py:494
  538.5 15.7 %collective-permute-start.17 = (bf16[4,128,256]{2,1,0:T(8,128)(2,1)S(1)}, bf16[4,128,256]{2,1,0:T(8,128)(2,1)S(1)}, u32[]{:S(2)}, u32[]{:S(2)}) collective-permute-start(bf16[4,128,256]{2,1,0:T(8,128)(2,1)S(1)} %dynamic-slice_convert_fusion.5), channel_id=1, source_target_pairs={{0,2},{2,0},{1,3},{3,1},{4,6},{6,4},{5,7},{7,5},{8,10},{10,8},{9,1... | collective-permute-start | bytes 786440 | tf_op jit(solution)/shard_map/ppermute | solution.py:489
  545.2 32.5 %slice-start.4 = ((s8[7012352]{0:T(1024)(128)(4,1)}), s8[4194304]{0:T(1024)(128)(4,1)S(1)}, s32[]{:S(2)}) async-start(s8[7012352]{0:T(1024)(128)(4,1)} %bitcast.215), calls=%async_computation.4 | async-start | bytes 8388608
  545.4 9.0 %collective-permute-start.22 = (bf16[4,128,256]{2,1,0:T(8,128)(2,1)S(1)}, bf16[4,128,256]{2,1,0:T(8,128)(2,1)S(1)}, u32[]{:S(2)}, u32[]{:S(2)}) collective-permute-start(bf16[4,128,256]{2,1,0:T(8,128)(2,1)S(1)} %fusion.54), channel_id=1, source_target_pairs={{0,4},{4,0},{1,5},{5,1},{2,6},{6,2},{3,7},{7,3},{8,12},{12,8},{9,1... | collective-permute-start | bytes 786440 | tf_op jit(solution)/shard_map/ppermute | solution.py:494
  550.9 23.6 %copy-start.18 = (f32[4,128,256]{2,1,0:T(8,128)S(1)}, f32[4,128,256]{2,1,0:T(8,128)}, u32[]{:S(2)}) copy-start(f32[4,128,256]{2,1,0:T(8,128)} %param.17) | copy-start | bytes 1572868
  550.9 23.6 %copy-start.34 = (f32[4,128,256]{2,1,0:T(8,128)S(1)}, f32[4,128,256]{2,1,0:T(8,128)}, u32[]{:S(2)}) copy-start(f32[4,128,256]{2,1,0:T(8,128)} %param.18) | copy-start | bytes 1572868
  550.9 23.6 %copy-start.35 = (f32[4,128,256]{2,1,0:T(8,128)S(1)}, f32[4,128,256]{2,1,0:T(8,128)}, u32[]{:S(2)}) copy-start(f32[4,128,256]{2,1,0:T(8,128)} %param.19) | copy-start | bytes 1572868
  550.9 6.5 collective-permute-start.8
  551.1 7.7 %collective-permute-start.13 = (bf16[128,256]{1,0:T(8,128)(2,1)S(1)}, bf16[128,256]{1,0:T(8,128)(2,1)S(1)}, u32[]{:S(2)}, u32[]{:S(2)}) collective-permute-start(bf16[128,256]{1,0:T(8,128)(2,1)S(1)} %fusion.71), channel_id=1, source_target_pairs={{0,8},{8,16},{16,24},{24,0},{1,9},{9,17},{17,25},{25,1},{2,10},{10... | collective-permute-start | bytes 196616 | tf_op jit(solution)/shard_map/ppermute | solution.py:501
  554.3 23.4 %slice-start.5 = ((s8[7012352]{0:T(1024)(128)(4,1)}), s8[2818048]{0:T(1024)(128)(4,1)S(1)}, s32[]{:S(2)}) async-start(s8[7012352]{0:T(1024)(128)(4,1)} %bitcast.215), calls=%async_computation.5 | async-start | bytes 5636096
  554.3 23.4 %copy-start.42 = (f32[1,1024]{1,0:T(1,128)S(1)}, f32[1,1024]{1,0:T(1,128)}, u32[]{:S(2)}) copy-start(f32[1,1024]{1,0:T(1,128)} %copy-done.41) | copy-start | bytes 12292
  554.3 6.8 %collective-permute-start.18 = (bf16[128,256]{1,0:T(8,128)(2,1)S(1)}, bf16[128,256]{1,0:T(8,128)(2,1)S(1)}, u32[]{:S(2)}, u32[]{:S(2)}) collective-permute-start(bf16[128,256]{1,0:T(8,128)(2,1)S(1)} %fusion.72), channel_id=1, source_target_pairs={{0,8},{8,16},{16,24},{24,0},{1,9},{9,17},{17,25},{25,1},{2,10},{10... | collective-permute-start | bytes 196616 | tf_op jit(solution)/shard_map/ppermute | solution.py:501
  554.5 7.5 %collective-permute-start.23 = (bf16[128,256]{1,0:T(8,128)(2,1)S(1)}, bf16[128,256]{1,0:T(8,128)(2,1)S(1)}, u32[]{:S(2)}, u32[]{:S(2)}) collective-permute-start(bf16[128,256]{1,0:T(8,128)(2,1)S(1)} %fusion.73), channel_id=1, source_target_pairs={{0,8},{8,16},{16,24},{24,0},{1,9},{9,17},{17,25},{25,1},{2,10},{10... | collective-permute-start | bytes 196616 | tf_op jit(solution)/shard_map/ppermute | solution.py:501
  557.4 6.8 %collective-permute-start.9 = (bf16[128,256]{1,0:T(8,128)(2,1)S(1)}, bf16[128,256]{1,0:T(8,128)(2,1)S(1)}, u32[]{:S(2)}, u32[]{:S(2)}) collective-permute-start(bf16[128,256]{1,0:T(8,128)(2,1)S(1)} %fusion.68), channel_id=1, source_target_pairs={{0,8},{8,16},{16,24},{24,0},{1,9},{9,17},{17,25},{25,1},{2,10},{10... | collective-permute-start | bytes 196616 | tf_op jit(solution)/shard_map/ppermute | solution.py:501
  558.8 6.8 %collective-permute-start.14 = (bf16[128,256]{1,0:T(8,128)(2,1)S(1)}, bf16[128,256]{1,0:T(8,128)(2,1)S(1)}, u32[]{:S(2)}, u32[]{:S(2)}) collective-permute-start(bf16[128,256]{1,0:T(8,128)(2,1)S(1)} %fusion.65), channel_id=1, source_target_pairs={{0,8},{8,16},{16,24},{24,0},{1,9},{9,17},{17,25},{25,1},{2,10},{10... | collective-permute-start | bytes 196616 | tf_op jit(solution)/shard_map/ppermute | solution.py:501
  561.2 6.4 collective-permute-start.19
  562.0 6.3 collective-permute-start.24
  564.3 6.6 %collective-permute-start.10 = (bf16[128,256]{1,0:T(8,128)(2,1)S(1)}, bf16[128,256]{1,0:T(8,128)(2,1)S(1)}, u32[]{:S(2)}, u32[]{:S(2)}) collective-permute-start(bf16[128,256]{1,0:T(8,128)(2,1)S(1)} %fusion.67), channel_id=1, source_target_pairs={{0,8},{8,16},{16,24},{24,0},{1,9},{9,17},{17,25},{25,1},{2,10},{10... | collective-permute-start | bytes 196616 | tf_op jit(solution)/shard_map/ppermute | solution.py:501
  565.7 6.1 collective-permute-start.15
  567.6 6.1 collective-permute-start.20
  568.3 6.1 collective-permute-start.25
  577.7 44.4 %copy-start.40 = (f32[1712]{0:T(1024)S(1)}, f32[1712]{0:T(1024)}, u32[]{:S(2)}) copy-start(f32[1712]{0:T(1024)} %copy-done.39) | copy-start | bytes 20548
  629.3 19.7 %copy-start.49 = (pred[176]{0:T(512)(128)(4,1)S(1)}, pred[176]{0:T(512)(128)(4,1)}, u32[]{:S(2)}) copy-start(pred[176]{0:T(512)(128)(4,1)} %add_compare_fusion) | copy-start | bytes 532
  629.9 19.1 %collective-permute-start.5 = (f32[176,1024]{1,0:T(8,128)S(1)}, f32[176,1024]{1,0:T(8,128)S(1)}, u32[]{:S(2)}, u32[]{:S(2)}) collective-permute-start(f32[176,1024]{1,0:T(8,128)S(1)} %slice.228), channel_id=1, source_target_pairs={{2,0},{3,1},{6,4},{7,5},{10,8},{11,9},{14,12},{15,13},{18,16},{19,... | collective-permute-start | bytes 2162696 | tf_op jit(solution)/shard_map/ppermute | solution.py:623
  (42 other events, 171.7 us)
